TPU v7x, 512 devices: a whole 4x4x16 slice. The times are simulated.
512 devices in a mesh: group: 4 (over z_hi, core), gx: 32 (over z_lo, y), gy: 4 (over x).
Axes of the slice: x: 4, y: 4, z: 16 (z_hi: 2, z_lo: 8; z = z_hi * 8 + z_lo), core: 2. Of those that a mesh axis runs over, the one named last changes fastest.
Arguments:
- parent_mass: float32 [512, 512, 512], P('gx', ('group', 'gy')), may hold values from -6 to 6
- fine_mass: float32 [512, 128, 128], P('gx', ('group', 'gy')), may hold values from -6 to 6
- offsets: int32 [3], replicated, may hold values from 0 to 511
Outputs:
- parent_potential: float32 [512, 512, 512], P('gx', ('group', 'gy'))
- fine_potential: float32 [512, 128, 128], P('gx', ('group', 'gy'))
All inputs are finite; a program needn't handle non-finite values.
Results may differ from a plain program's by a relative error of at most 0.0003.
Values sent between devices are 32-bit elements; how exact they have to be, the bound alone decides.
No kernel may reach another device: no remote copies, remote signals or barrier semaphores. Data moves between devices by JAX's collectives and lax.ppermute only.
A program may use at most 128 MiB of HBM per device.

v0:
```python
import math
import jax
import jax.numpy as jnp
from jax import lax
from jax.sharding import PartitionSpec as P

NP = 512
CYCLES = 2
LEVELS = 3
SWEEPS = 2
COARSE_SWEEPS = 4
OMEGA = 6.0 / 7.0
HIGH = lax.Precision.HIGHEST


def extended(shard, sides, width):
    edges = {}
    for axis, dim in sides:
        size, length = (lax.axis_size(axis), shard.shape[dim])
        up = [(i, (i + 1) % size) for i in range(size - 1)]
        last = lax.slice_in_dim(shard, length - width, length, axis=dim)
        initial = lax.slice_in_dim(shard, 0, width, axis=dim)
        edges[dim] = (
            lax.ppermute(last, axis, up),
            lax.ppermute(initial, axis, [(b, a) for a, b in up]),
        )
    done = []
    for _, dim in sides:
        low, high = edges[dim]
        around = [(width, width) if d in done else (0, 0) for d in range(shard.ndim)]
        shard = jnp.concatenate([jnp.pad(low, around), shard, jnp.pad(high, around)], axis=dim)
        done.append(dim)
    return shard


def cas_table(wave, places, length):
    phase = wave[:, None] * places[None, :] % length
    angle = phase.astype(jnp.float32) * (2.0 * math.pi / length)
    return jnp.cos(angle) + jnp.sin(angle)


def eigen_of(wave, length):
    sine = jnp.sin(wave.astype(jnp.float32) * (math.pi / length))
    return 4.0 * sine * sine


def green(wave_a, wave_b, wave_c):
    lam = (
        eigen_of(wave_a, NP)[:, None, None]
        + eigen_of(wave_b, NP)[None, :, None]
        + eigen_of(wave_c, NP)[None, None, :]
    )
    inverse = jnp.where(lam > 0, 1.0 / jnp.where(lam > 0, lam, 1.0), 0.0)
    return inverse * (1.0 / float(NP**3))


def last_axis(block, table):
    return jnp.einsum("abj,kj->abk", block, table, precision=HIGH)


def middle_axis(block, table):
    return jnp.einsum("ajc,kj->akc", block, table, precision=HIGH)


def first_axis(block, table):
    product = jnp.dot(table, block.reshape(block.shape[0], -1), precision=HIGH)
    return product.reshape((table.shape[0],) + block.shape[1:])


def coarsen(block):
    a, b, c = block.shape
    return block.reshape(a // 2, 2, b // 2, 2, c // 2, 2).sum(axis=(1, 3, 5))


def refine(block):
    return jnp.repeat(jnp.repeat(jnp.repeat(block, 2, axis=0), 2, axis=1), 2, axis=2)


def stencil(field, padded):
    beside = padded[2:, 1:-1, 1:-1] + padded[:-2, 1:-1, 1:-1]
    beside = beside + padded[1:-1, 2:, 1:-1] + padded[1:-1, :-2, 1:-1]
    beside = beside + padded[1:-1, 1:-1, 2:] + padded[1:-1, 1:-1, :-2]
    return 6.0 * field - beside


def operate(field, edge, flags):
    padded = extended(field, (("gx", 0), (("group", "gy"), 1)), 1)
    if edge:
        padded = padded.at[0, 1:-1].set(jnp.where(flags[0], field[0], padded[0, 1:-1]))
        padded = padded.at[-1, 1:-1].set(jnp.where(flags[1], field[-1], padded[-1, 1:-1]))
        padded = padded.at[1:-1, 0].set(jnp.where(flags[2], field[:, 0], padded[1:-1, 0]))
        padded = padded.at[1:-1, -1].set(jnp.where(flags[3], field[:, -1], padded[1:-1, -1]))
        padded = jnp.pad(padded, ((0, 0), (0, 0), (1, 1)), mode="edge")
    else:
        padded = jnp.pad(padded, ((0, 0), (0, 0), (1, 1)))
    return stencil(field, padded)


def smooth(corr, resid, sweeps, flags):
    for turn in range(sweeps):
        if corr is None:
            corr = OMEGA / 6.0 * resid
        else:
            corr = corr + OMEGA / 6.0 * (resid - operate(corr, False, flags))
    return corr


def coarsest(resid, flags):
    return smooth(None, resid, COARSE_SWEEPS, flags)


def cycle(corr, resid, level, flags, index_x, index_y):
    if level == LEVELS - 1:
        return coarsest(resid, flags)
    corr = smooth(corr, resid, SWEEPS, flags)
    lower = 0.5 * coarsen(resid - operate(corr, False, flags))
    below = cycle(None, lower, level + 1, flags, index_x, index_y)
    corr = corr + refine(below)
    return smooth(corr, resid, SWEEPS, flags)


def local(parent_mass, fine_mass, offsets):
    count_x = lax.axis_size("gx")
    count_y = lax.axis_size(("group", "gy"))
    index_x = lax.axis_index("gx")
    index_y = lax.axis_index(("group", "gy"))
    wave = jnp.arange(NP, dtype=jnp.int32)
    full = cas_table(wave, wave, NP)
    rest = coarsen(fine_mass)
    span_x = rest.shape[0] * count_x
    span_y = rest.shape[1] * count_y
    x_table = cas_table(wave, offsets[0] + jnp.arange(span_x, dtype=jnp.int32), NP)
    y_table = cas_table(wave, offsets[1] + jnp.arange(span_y, dtype=jnp.int32), NP)
    z_table = cas_table(wave, offsets[2] + jnp.arange(rest.shape[2], dtype=jnp.int32), NP)
    dense = last_axis(parent_mass, full)
    light = last_axis(rest, z_table)
    dense, light = (
        lax.all_to_all(dense, "gx", split_axis=2, concat_axis=0, tiled=True),
        lax.all_to_all(light, "gx", split_axis=2, concat_axis=0, tiled=True),
    )
    dense = first_axis(dense, full)
    light = first_axis(light, x_table)
    dense, light = (
        lax.all_to_all(dense, ("group", "gy"), split_axis=0, concat_axis=1, tiled=True),
        lax.all_to_all(light, ("group", "gy"), split_axis=0, concat_axis=1, tiled=True),
    )
    spectrum = middle_axis(dense, full) + middle_axis(light, y_table)
    width_a = spectrum.shape[0]
    width_c = spectrum.shape[2]
    spectrum = spectrum * green(
        index_y * width_a + jnp.arange(width_a, dtype=jnp.int32),
        wave,
        index_x * width_c + jnp.arange(width_c, dtype=jnp.int32),
    )
    whole = middle_axis(spectrum, full)
    near = middle_axis(spectrum, y_table.T)
    whole, near = (
        lax.all_to_all(whole, ("group", "gy"), split_axis=1, concat_axis=0, tiled=True),
        lax.all_to_all(near, ("group", "gy"), split_axis=1, concat_axis=0, tiled=True),
    )
    whole = first_axis(whole, full)
    near = first_axis(near, x_table.T)
    whole, near = (
        lax.all_to_all(whole, "gx", split_axis=0, concat_axis=2, tiled=True),
        lax.all_to_all(near, "gx", split_axis=0, concat_axis=2, tiled=True),
    )
    potential = last_axis(whole, full)
    footprint = last_axis(near, z_table.T)
    flags = (index_x == 0, index_x == count_x - 1, index_y == 0, index_y == count_y - 1)
    start = refine(footprint)
    resid = 2.0 * fine_mass - operate(start, True, flags)
    corr = None
    for turn in range(CYCLES):
        corr = cycle(corr, resid, 0, flags, index_x, index_y)
    return (potential, start + corr)


def solution(mesh):
    return jax.shard_map(
        local,
        mesh=mesh,
        in_specs=(P("gx", ("group", "gy"), None), P("gx", ("group", "gy"), None), P()),
        out_specs=(P("gx", ("group", "gy"), None), P("gx", ("group", "gy"), None)),
        check_vma=False,
    )
```

profile of v0, /device:TPU:135, one launch (start us, length us, event | category | flops | bytes accessed | tf_op | source)
XLA Modules:
  0.0 1045.0 jit_solution(9459610186346306558)
XLA Ops:
  0.7 6.4 reshape.326
  13.9 13.5 %all-to-all-start.2 = ((f32[32,1,512]{2,1,0:T(1,128)}), f32[32,1,512]{2,1,0:T(1,128)S(1)}, u32[]{:S(2)}, u32[]{:S(2)}) async-start(f32[32,1,512]{2,1,0:T(1,128)} %reshape.359), calls=%async_computation.2 | async-start | bytes 131072 | tf_op jit(solution)/shard_map/all_to_all | solution.py:139
  27.4 6.7 convolution_bitcast_fusion.1
  37.8 4.7 reshape.355
  42.5 12.6 %all-to-all-start = ((f32[32,1,8192]{2,1,0:T(1,128)}), f32[32,1,8192]{2,1,0:T(1,128)S(1)}, u32[]{:S(2)}, u32[]{:S(2)}) async-start(f32[32,1,8192]{2,1,0:T(1,128)} %reshape.355), calls=%async_computation | async-start | bytes 2097152 | tf_op jit(solution)/shard_map/all_to_all | solution.py:138
  64.1 37.1 %all-to-all-done = f32[32,1,8192]{2,1,0:T(1,128)S(1)} async-done(((f32[32,1,8192]{2,1,0:T(1,128)}), f32[32,1,8192]{2,1,0:T(1,128)S(1)}, u32[]{:S(2)}, u32[]{:S(2)}) %all-to-all-start) | async-done | bytes 1048608 | tf_op jit(solution)/shard_map/all_to_all | solution.py:138
  101.2 11.4 %all-to-all-start.3 = ((f32[16,1,2048]{2,1,0:T(1,128)}), f32[16,1,2048]{2,1,0:T(1,128)S(1)}, u32[]{:S(2)}, u32[]{:S(2)}) async-start(f32[16,1,2048]{2,1,0:T(1,128)} %reshape.361), calls=%async_computation.3 | async-start | bytes 262144 | tf_op jit(solution)/shard_map/all_to_all | solution.py:145
  118.7 7.0 copy.590
  125.7 7.8 reshape.325
  133.8 6.4 fusion.15
  143.8 4.7 reshape.357
  148.6 14.7 %all-to-all-start.1 = ((f32[16,1,16384]{2,1,0:T(1,128)}), f32[16,1,16384]{2,1,0:T(1,128)S(1)}, u32[]{:S(2)}, u32[]{:S(2)}) async-start(f32[16,1,16384]{2,1,0:T(1,128)} %reshape.357), calls=%async_computation.1 | async-start | bytes 2097152 | tf_op jit(solution)/shard_map/all_to_all | solution.py:144
  167.2 50.5 %all-to-all-done.1 = f32[16,1,16384]{2,1,0:T(1,128)S(1)} async-done(((f32[16,1,16384]{2,1,0:T(1,128)}), f32[16,1,16384]{2,1,0:T(1,128)S(1)}, u32[]{:S(2)}, u32[]{:S(2)}) %all-to-all-start.1) | async-done | bytes 1048608 | tf_op jit(solution)/shard_map/all_to_all | solution.py:144
  223.6 6.6 copy.655
  233.9 7.1 fusion.13
  244.9 18.9 %all_to_all.132 = f32[16,1,2048]{2,1,0:T(1,128)S(1)} all-to-all(f32[16,1,2048]{2,1,0:T(1,128)S(1)} %reshape.367), channel_id=1, replica_groups=mesh['group'=4,'gx'=32,'gy'=4] {'group','gy'}, dimensions={0} | all-to-all | bytes 262144 | tf_op jit(solution)/shard_map/all_to_all | solution.py:159
  269.4 12.1 %all-to-all-start.7 = ((f32[32,1,512]{2,1,0:T(1,128)}), f32[32,1,512]{2,1,0:T(1,128)S(1)}, u32[]{:S(2)}, u32[]{:S(2)}) async-start(f32[32,1,512]{2,1,0:T(1,128)} %reshape.369), calls=%async_computation.7 | async-start | bytes 131072 | tf_op jit(solution)/shard_map/all_to_all | solution.py:165
  282.1 6.4 all-to-all-done.7
  296.7 13.6 %collective-permute-start = (f32[16,1,128]{2,1,0:T(1,128)S(1)}, f32[16,1,128]{2,1,0:T(1,128)S(1)}, u32[]{:S(2)}, u32[]{:S(2)}) collective-permute-start(f32[16,1,128]{2,1,0:T(1,128)S(1)} %get-tuple-element.98), channel_id=1, source_target_pairs={{0,1},{1,2},{2,3},{3,128},{128,129},{129,130},{130,131},{131,256},... | collective-permute-start | bytes 24584 | tf_op jit(solution)/shard_map/ppermute | solution.py:24
  310.4 6.4 collective-permute-start.2
  321.5 14.5 %collective-permute-start.7 = (f32[16,1,128]{2,1,0:T(1,128)S(1)}, f32[16,1,128]{2,1,0:T(1,128)S(1)}, u32[]{:S(2)}, u32[]{:S(2)}) collective-permute-start(f32[16,1,128]{2,1,0:T(1,128)S(1)} %get-tuple-element.96), channel_id=1, source_target_pairs={{0,1},{1,2},{2,3},{3,128},{128,129},{129,130},{130,131},{131,256},... | collective-permute-start | bytes 24584 | tf_op jit(solution)/shard_map/ppermute | solution.py:24
  336.0 6.9 collective-permute-start.4
  344.9 5.7 collective-permute-done.5
  352.9 14.5 %collective-permute-start.11 = (f32[16,1,128]{2,1,0:T(1,128)S(1)}, f32[16,1,128]{2,1,0:T(1,128)S(1)}, u32[]{:S(2)}, u32[]{:S(2)}) collective-permute-start(f32[16,1,128]{2,1,0:T(1,128)S(1)} %get-tuple-element.92), channel_id=1, source_target_pairs={{0,1},{1,2},{2,3},{3,128},{128,129},{129,130},{130,131},{131,256},... | collective-permute-start | bytes 24584 | tf_op jit(solution)/shard_map/ppermute | solution.py:24
  372.9 4.2 collective-permute-done.9
  377.5 5.5 reshape.335
  387.5 14.5 %collective-permute-start.15 = (f32[8,1,64]{2,1,0:T(1,128)S(1)}, f32[8,1,64]{2,1,0:T(1,128)S(1)}, u32[]{:S(2)}, u32[]{:S(2)}) collective-permute-start(f32[8,1,64]{2,1,0:T(1,128)S(1)} %get-tuple-element.132), channel_id=1, source_target_pairs={{0,1},{1,2},{2,3},{3,128},{128,129},{129,130},{130,131},{131,256},... | collective-permute-start | bytes 6152 | tf_op jit(solution)/shard_map/ppermute | solution.py:24
  413.7 14.5 %collective-permute-start.19 = (f32[8,1,64]{2,1,0:T(1,128)S(1)}, f32[8,1,64]{2,1,0:T(1,128)S(1)}, u32[]{:S(2)}, u32[]{:S(2)}) collective-permute-start(f32[8,1,64]{2,1,0:T(1,128)S(1)} %get-tuple-element.128), channel_id=1, source_target_pairs={{0,1},{1,2},{2,3},{3,128},{128,129},{129,130},{130,131},{131,256},... | collective-permute-start | bytes 6152 | tf_op jit(solution)/shard_map/ppermute | solution.py:24
  440.6 14.5 %collective-permute-start.23 = (f32[4,1,32]{2,0,1:T(4,128)S(1)}, f32[4,1,32]{2,0,1:T(4,128)S(1)}, u32[]{:S(2)}, u32[]{:S(2)}) collective-permute-start(f32[4,1,32]{2,0,1:T(4,128)S(1)} %get-tuple-element.156), channel_id=1, source_target_pairs={{0,1},{1,2},{2,3},{3,128},{128,129},{129,130},{130,131},{131,256},... | collective-permute-start | bytes 1544 | tf_op jit(solution)/shard_map/ppermute | solution.py:24
  466.7 14.5 %collective-permute-start.27 = (f32[4,1,32]{2,0,1:T(4,128)S(1)}, f32[4,1,32]{2,0,1:T(4,128)S(1)}, u32[]{:S(2)}, u32[]{:S(2)}) collective-permute-start(f32[4,1,32]{2,0,1:T(4,128)S(1)} %get-tuple-element.152), channel_id=1, source_target_pairs={{0,1},{1,2},{2,3},{3,128},{128,129},{129,130},{130,131},{131,256},... | collective-permute-start | bytes 1544 | tf_op jit(solution)/shard_map/ppermute | solution.py:24
  492.9 14.5 %collective-permute-start.31 = (f32[4,1,32]{2,0,1:T(4,128)S(1)}, f32[4,1,32]{2,0,1:T(4,128)S(1)}, u32[]{:S(2)}, u32[]{:S(2)}) collective-permute-start(f32[4,1,32]{2,0,1:T(4,128)S(1)} %get-tuple-element.148), channel_id=1, source_target_pairs={{0,1},{1,2},{2,3},{3,128},{128,129},{129,130},{130,131},{131,256},... | collective-permute-start | bytes 1544 | tf_op jit(solution)/shard_map/ppermute | solution.py:24
  519.3 14.5 %collective-permute-start.35 = (f32[8,1,64]{2,1,0:T(1,128)S(1)}, f32[8,1,64]{2,1,0:T(1,128)S(1)}, u32[]{:S(2)}, u32[]{:S(2)}) collective-permute-start(f32[8,1,64]{2,1,0:T(1,128)S(1)} %get-tuple-element.124), channel_id=1, source_target_pairs={{0,1},{1,2},{2,3},{3,128},{128,129},{129,130},{130,131},{131,256},... | collective-permute-start | bytes 6152 | tf_op jit(solution)/shard_map/ppermute | solution.py:24
  545.5 14.5 %collective-permute-start.39 = (f32[8,1,64]{2,1,0:T(1,128)S(1)}, f32[8,1,64]{2,1,0:T(1,128)S(1)}, u32[]{:S(2)}, u32[]{:S(2)}) collective-permute-start(f32[8,1,64]{2,1,0:T(1,128)S(1)} %get-tuple-element.120), channel_id=1, source_target_pairs={{0,1},{1,2},{2,3},{3,128},{128,129},{129,130},{130,131},{131,256},... | collective-permute-start | bytes 6152 | tf_op jit(solution)/shard_map/ppermute | solution.py:24
  572.2 14.5 %collective-permute-start.43 = (f32[16,1,128]{2,1,0:T(1,128)S(1)}, f32[16,1,128]{2,1,0:T(1,128)S(1)}, u32[]{:S(2)}, u32[]{:S(2)}) collective-permute-start(f32[16,1,128]{2,1,0:T(1,128)S(1)} %get-tuple-element.88), channel_id=1, source_target_pairs={{0,1},{1,2},{2,3},{3,128},{128,129},{129,130},{130,131},{131,256},... | collective-permute-start | bytes 24584 | tf_op jit(solution)/shard_map/ppermute | solution.py:24
  592.1 4.2 collective-permute-done.41
  598.6 14.5 %collective-permute-start.47 = (f32[16,1,128]{2,1,0:T(1,128)S(1)}, f32[16,1,128]{2,1,0:T(1,128)S(1)}, u32[]{:S(2)}, u32[]{:S(2)}) collective-permute-start(f32[16,1,128]{2,1,0:T(1,128)S(1)} %get-tuple-element.84), channel_id=1, source_target_pairs={{0,1},{1,2},{2,3},{3,128},{128,129},{129,130},{130,131},{131,256},... | collective-permute-start | bytes 24584 | tf_op jit(solution)/shard_map/ppermute | solution.py:24
  618.4 4.2 collective-permute-done.45
  624.9 14.5 %collective-permute-start.51 = (f32[16,1,128]{2,1,0:T(1,128)S(1)}, f32[16,1,128]{2,1,0:T(1,128)S(1)}, u32[]{:S(2)}, u32[]{:S(2)}) collective-permute-start(f32[16,1,128]{2,1,0:T(1,128)S(1)} %get-tuple-element.80), channel_id=1, source_target_pairs={{0,1},{1,2},{2,3},{3,128},{128,129},{129,130},{130,131},{131,256},... | collective-permute-start | bytes 24584 | tf_op jit(solution)/shard_map/ppermute | solution.py:24
  651.3 14.5 %collective-permute-start.55 = (f32[16,1,128]{2,1,0:T(1,128)S(1)}, f32[16,1,128]{2,1,0:T(1,128)S(1)}, u32[]{:S(2)}, u32[]{:S(2)}) collective-permute-start(f32[16,1,128]{2,1,0:T(1,128)S(1)} %get-tuple-element.76), channel_id=1, source_target_pairs={{0,1},{1,2},{2,3},{3,128},{128,129},{129,130},{130,131},{131,256},... | collective-permute-start | bytes 24584 | tf_op jit(solution)/shard_map/ppermute | solution.py:24
  671.3 6.7 convolution_bitcast_fusion
  681.7 4.7 reshape.363
  686.4 4.2 all-to-all-start.4
  693.6 13.9 %collective-permute-start.59 = (f32[16,1,128]{2,1,0:T(1,128)S(1)}, f32[16,1,128]{2,1,0:T(1,128)S(1)}, u32[]{:S(2)}, u32[]{:S(2)}) collective-permute-start(f32[16,1,128]{2,1,0:T(1,128)S(1)} %get-tuple-element.72), channel_id=1, source_target_pairs={{0,1},{1,2},{2,3},{3,128},{128,129},{129,130},{130,131},{131,256},... | collective-permute-start | bytes 24584 | tf_op jit(solution)/shard_map/ppermute | solution.py:24
  707.5 5.2 collective-permute-start.56
  714.7 6.1 collective-permute-done.57
  721.1 5.5 reshape.343
  731.1 14.5 %collective-permute-start.63 = (f32[8,1,64]{2,1,0:T(1,128)S(1)}, f32[8,1,64]{2,1,0:T(1,128)S(1)}, u32[]{:S(2)}, u32[]{:S(2)}) collective-permute-start(f32[8,1,64]{2,1,0:T(1,128)S(1)} %get-tuple-element.116), channel_id=1, source_target_pairs={{0,1},{1,2},{2,3},{3,128},{128,129},{129,130},{130,131},{131,256},... | collective-permute-start | bytes 6152 | tf_op jit(solution)/shard_map/ppermute | solution.py:24
  751.0 10.6 %collective-permute-done.61 = f32[1,4,64]{2,1,0:T(4,128)S(1)} collective-permute-done((f32[1,4,64]{2,1,0:T(4,128)S(1)}, f32[1,4,64]{2,1,0:T(4,128)S(1)}, u32[]{:S(2)}, u32[]{:S(2)}) %collective-permute-start.61) | collective-permute-done | bytes 1056 | tf_op jit(solution)/shard_map/ppermute | solution.py:24
  763.7 14.5 %collective-permute-start.67 = (f32[8,1,64]{2,1,0:T(1,128)S(1)}, f32[8,1,64]{2,1,0:T(1,128)S(1)}, u32[]{:S(2)}, u32[]{:S(2)}) collective-permute-start(f32[8,1,64]{2,1,0:T(1,128)S(1)} %get-tuple-element.112), channel_id=1, source_target_pairs={{0,1},{1,2},{2,3},{3,128},{128,129},{129,130},{130,131},{131,256},... | collective-permute-start | bytes 6152 | tf_op jit(solution)/shard_map/ppermute | solution.py:24
  784.2 5.7 collective-permute-done.65
  792.7 14.5 %collective-permute-start.71 = (f32[4,1,32]{2,0,1:T(4,128)S(1)}, f32[4,1,32]{2,0,1:T(4,128)S(1)}, u32[]{:S(2)}, u32[]{:S(2)}) collective-permute-start(f32[4,1,32]{2,0,1:T(4,128)S(1)} %get-tuple-element.144), channel_id=1, source_target_pairs={{0,1},{1,2},{2,3},{3,128},{128,129},{129,130},{130,131},{131,256},... | collective-permute-start | bytes 1544 | tf_op jit(solution)/shard_map/ppermute | solution.py:24
  818.9 14.5 %collective-permute-start.75 = (f32[4,1,32]{2,0,1:T(4,128)S(1)}, f32[4,1,32]{2,0,1:T(4,128)S(1)}, u32[]{:S(2)}, u32[]{:S(2)}) collective-permute-start(f32[4,1,32]{2,0,1:T(4,128)S(1)} %get-tuple-element.140), channel_id=1, source_target_pairs={{0,1},{1,2},{2,3},{3,128},{128,129},{129,130},{130,131},{131,256},... | collective-permute-start | bytes 1544 | tf_op jit(solution)/shard_map/ppermute | solution.py:24
  849.3 6.6 copy.654
  859.5 6.4 fusion.10
  869.6 4.9 reshape.365
  874.5 8.4 all-to-all-start.5
  884.9 14.5 %collective-permute-start.79 = (f32[4,1,32]{2,0,1:T(4,128)S(1)}, f32[4,1,32]{2,0,1:T(4,128)S(1)}, u32[]{:S(2)}, u32[]{:S(2)}) collective-permute-start(f32[4,1,32]{2,0,1:T(4,128)S(1)} %get-tuple-element.136), channel_id=1, source_target_pairs={{0,1},{1,2},{2,3},{3,128},{128,129},{129,130},{130,131},{131,256},... | collective-permute-start | bytes 1544 | tf_op jit(solution)/shard_map/ppermute | solution.py:24
  899.4 4.3 collective-permute-start.76
  906.2 5.2 collective-permute-done.77
  913.7 14.5 %collective-permute-start.83 = (f32[8,1,64]{2,1,0:T(1,128)S(1)}, f32[8,1,64]{2,1,0:T(1,128)S(1)}, u32[]{:S(2)}, u32[]{:S(2)}) collective-permute-start(f32[8,1,64]{2,1,0:T(1,128)S(1)} %get-tuple-element.108), channel_id=1, source_target_pairs={{0,1},{1,2},{2,3},{3,128},{128,129},{129,130},{130,131},{131,256},... | collective-permute-start | bytes 6152 | tf_op jit(solution)/shard_map/ppermute | solution.py:24
  939.9 14.5 %collective-permute-start.87 = (f32[8,1,64]{2,1,0:T(1,128)S(1)}, f32[8,1,64]{2,1,0:T(1,128)S(1)}, u32[]{:S(2)}, u32[]{:S(2)}) collective-permute-start(f32[8,1,64]{2,1,0:T(1,128)S(1)} %get-tuple-element.104), channel_id=1, source_target_pairs={{0,1},{1,2},{2,3},{3,128},{128,129},{129,130},{130,131},{131,256},... | collective-permute-start | bytes 6152 | tf_op jit(solution)/shard_map/ppermute | solution.py:24
  966.7 14.5 %collective-permute-start.91 = (f32[16,1,128]{2,1,0:T(1,128)S(1)}, f32[16,1,128]{2,1,0:T(1,128)S(1)}, u32[]{:S(2)}, u32[]{:S(2)}) collective-permute-start(f32[16,1,128]{2,1,0:T(1,128)S(1)} %get-tuple-element.68), channel_id=1, source_target_pairs={{0,1},{1,2},{2,3},{3,128},{128,129},{129,130},{130,131},{131,256},... | collective-permute-start | bytes 24584 | tf_op jit(solution)/shard_map/ppermute | solution.py:24
  993.0 14.5 %collective-permute-start.95 = (f32[16,1,128]{2,1,0:T(1,128)S(1)}, f32[16,1,128]{2,1,0:T(1,128)S(1)}, u32[]{:S(2)}, u32[]{:S(2)}) collective-permute-start(f32[16,1,128]{2,1,0:T(1,128)S(1)} %get-tuple-element.64), channel_id=1, source_target_pairs={{0,1},{1,2},{2,3},{3,128},{128,129},{129,130},{130,131},{131,256},... | collective-permute-start | bytes 24584 | tf_op jit(solution)/shard_map/ppermute | solution.py:24
  1027.0 17.8 %fusion.8 = f32[16,32,512]{2,1,0:T(8,128)} fusion(f32[16,32,512]{1,2,0:T(8,128)S(1)} %bitcast.160), kind=kOutput, calls=%fused_computation.19 | convolution fusion | flops 1614544896 | bytes 2097152 | tf_op jit(solution)/shard_map/abj,kj->abk/dot_general | solution.py:58
  (433 shorter events, 321.4 us)
Async XLA Ops:
  13.9 28.6 %all-to-all-start.2 = ((f32[32,1,512]{2,1,0:T(1,128)}), f32[32,1,512]{2,1,0:T(1,128)S(1)}, u32[]{:S(2)}, u32[]{:S(2)}) async-start(f32[32,1,512]{2,1,0:T(1,128)} %reshape.359), calls=%async_computation.2 | async-start | bytes 131072 | tf_op jit(solution)/shard_map/all_to_all | solution.py:139
  42.5 58.7 %all-to-all-start = ((f32[32,1,8192]{2,1,0:T(1,128)}), f32[32,1,8192]{2,1,0:T(1,128)S(1)}, u32[]{:S(2)}, u32[]{:S(2)}) async-start(f32[32,1,8192]{2,1,0:T(1,128)} %reshape.355), calls=%async_computation | async-start | bytes 2097152 | tf_op jit(solution)/shard_map/all_to_all | solution.py:138
  101.2 47.3 %all-to-all-start.3 = ((f32[16,1,2048]{2,1,0:T(1,128)}), f32[16,1,2048]{2,1,0:T(1,128)S(1)}, u32[]{:S(2)}, u32[]{:S(2)}) async-start(f32[16,1,2048]{2,1,0:T(1,128)} %reshape.361), calls=%async_computation.3 | async-start | bytes 262144 | tf_op jit(solution)/shard_map/all_to_all | solution.py:145
  148.6 69.1 %all-to-all-start.1 = ((f32[16,1,16384]{2,1,0:T(1,128)}), f32[16,1,16384]{2,1,0:T(1,128)S(1)}, u32[]{:S(2)}, u32[]{:S(2)}) async-start(f32[16,1,16384]{2,1,0:T(1,128)} %reshape.357), calls=%async_computation.1 | async-start | bytes 2097152 | tf_op jit(solution)/shard_map/all_to_all | solution.py:144
  269.4 19.1 %all-to-all-start.7 = ((f32[32,1,512]{2,1,0:T(1,128)}), f32[32,1,512]{2,1,0:T(1,128)S(1)}, u32[]{:S(2)}, u32[]{:S(2)}) async-start(f32[32,1,512]{2,1,0:T(1,128)} %reshape.369), calls=%async_computation.7 | async-start | bytes 131072 | tf_op jit(solution)/shard_map/all_to_all | solution.py:165
  291.6 25.2 %collective-permute-start.1 = (f32[1,8,128]{2,1,0:T(8,128)S(1)}, f32[1,8,128]{2,1,0:T(8,128)S(1)}, u32[]{:S(2)}, u32[]{:S(2)}) collective-permute-start(f32[1,8,128]{2,1,0:T(8,128)S(1)} %copy.619), channel_id=1, source_target_pairs={{0,4},{4,8},{8,12},{12,16},{16,20},{20,24},{24,28},{28,32},{32,36}... | collective-permute-start | bytes 12296 | tf_op jit(solution)/shard_map/ppermute | solution.py:24
  293.8 23.7 %collective-permute-start.3 = (f32[16,1,128]{2,1,0:T(1,128)S(1)}, f32[16,1,128]{2,1,0:T(1,128)S(1)}, u32[]{:S(2)}, u32[]{:S(2)}) collective-permute-start(f32[16,1,128]{2,1,0:T(1,128)S(1)} %get-tuple-element.99), channel_id=1, source_target_pairs={{1,0},{2,1},{3,2},{128,3},{129,128},{130,129},{131,130},{256,131},... | collective-permute-start | bytes 24584 | tf_op jit(solution)/shard_map/ppermute | solution.py:25
  296.7 20.9 %collective-permute-start = (f32[16,1,128]{2,1,0:T(1,128)S(1)}, f32[16,1,128]{2,1,0:T(1,128)S(1)}, u32[]{:S(2)}, u32[]{:S(2)}) collective-permute-start(f32[16,1,128]{2,1,0:T(1,128)S(1)} %get-tuple-element.98), channel_id=1, source_target_pairs={{0,1},{1,2},{2,3},{3,128},{128,129},{129,130},{130,131},{131,256},... | collective-permute-start | bytes 24584 | tf_op jit(solution)/shard_map/ppermute | solution.py:24
  319.6 25.3 %collective-permute-start.6 = (f32[16,1,128]{2,1,0:T(1,128)S(1)}, f32[16,1,128]{2,1,0:T(1,128)S(1)}, u32[]{:S(2)}, u32[]{:S(2)}) collective-permute-start(f32[16,1,128]{2,1,0:T(1,128)S(1)} %get-tuple-element.97), channel_id=1, source_target_pairs={{1,0},{2,1},{3,2},{128,3},{129,128},{130,129},{131,130},{256,131},... | collective-permute-start | bytes 24584 | tf_op jit(solution)/shard_map/ppermute | solution.py:25
  321.5 23.4 %collective-permute-start.7 = (f32[16,1,128]{2,1,0:T(1,128)S(1)}, f32[16,1,128]{2,1,0:T(1,128)S(1)}, u32[]{:S(2)}, u32[]{:S(2)}) collective-permute-start(f32[16,1,128]{2,1,0:T(1,128)S(1)} %get-tuple-element.96), channel_id=1, source_target_pairs={{0,1},{1,2},{2,3},{3,128},{128,129},{129,130},{130,131},{131,256},... | collective-permute-start | bytes 24584 | tf_op jit(solution)/shard_map/ppermute | solution.py:24
  336.0 8.9 collective-permute-start.4
  342.9 7.7 collective-permute-start.5
  351.0 21.9 %collective-permute-start.10 = (f32[16,1,128]{2,1,0:T(1,128)S(1)}, f32[16,1,128]{2,1,0:T(1,128)S(1)}, u32[]{:S(2)}, u32[]{:S(2)}) collective-permute-start(f32[16,1,128]{2,1,0:T(1,128)S(1)} %get-tuple-element.93), channel_id=1, source_target_pairs={{1,0},{2,1},{3,2},{128,3},{129,128},{130,129},{131,130},{256,131},... | collective-permute-start | bytes 24584 | tf_op jit(solution)/shard_map/ppermute | solution.py:25
  352.9 20.0 %collective-permute-start.11 = (f32[16,1,128]{2,1,0:T(1,128)S(1)}, f32[16,1,128]{2,1,0:T(1,128)S(1)}, u32[]{:S(2)}, u32[]{:S(2)}) collective-permute-start(f32[16,1,128]{2,1,0:T(1,128)S(1)} %get-tuple-element.92), channel_id=1, source_target_pairs={{0,1},{1,2},{2,3},{3,128},{128,129},{129,130},{130,131},{131,256},... | collective-permute-start | bytes 24584 | tf_op jit(solution)/shard_map/ppermute | solution.py:24
  385.6 21.7 %collective-permute-start.14 = (f32[8,1,64]{2,1,0:T(1,128)S(1)}, f32[8,1,64]{2,1,0:T(1,128)S(1)}, u32[]{:S(2)}, u32[]{:S(2)}) collective-permute-start(f32[8,1,64]{2,1,0:T(1,128)S(1)} %get-tuple-element.133), channel_id=1, source_target_pairs={{1,0},{2,1},{3,2},{128,3},{129,128},{130,129},{131,130},{256,131},... | collective-permute-start | bytes 6152 | tf_op jit(solution)/shard_map/ppermute | solution.py:25
  387.5 19.8 %collective-permute-start.15 = (f32[8,1,64]{2,1,0:T(1,128)S(1)}, f32[8,1,64]{2,1,0:T(1,128)S(1)}, u32[]{:S(2)}, u32[]{:S(2)}) collective-permute-start(f32[8,1,64]{2,1,0:T(1,128)S(1)} %get-tuple-element.132), channel_id=1, source_target_pairs={{0,1},{1,2},{2,3},{3,128},{128,129},{129,130},{130,131},{131,256},... | collective-permute-start | bytes 6152 | tf_op jit(solution)/shard_map/ppermute | solution.py:24
  411.8 21.7 %collective-permute-start.18 = (f32[8,1,64]{2,1,0:T(1,128)S(1)}, f32[8,1,64]{2,1,0:T(1,128)S(1)}, u32[]{:S(2)}, u32[]{:S(2)}) collective-permute-start(f32[8,1,64]{2,1,0:T(1,128)S(1)} %get-tuple-element.129), channel_id=1, source_target_pairs={{1,0},{2,1},{3,2},{128,3},{129,128},{130,129},{131,130},{256,131},... | collective-permute-start | bytes 6152 | tf_op jit(solution)/shard_map/ppermute | solution.py:25
  413.7 19.8 %collective-permute-start.19 = (f32[8,1,64]{2,1,0:T(1,128)S(1)}, f32[8,1,64]{2,1,0:T(1,128)S(1)}, u32[]{:S(2)}, u32[]{:S(2)}) collective-permute-start(f32[8,1,64]{2,1,0:T(1,128)S(1)} %get-tuple-element.128), channel_id=1, source_target_pairs={{0,1},{1,2},{2,3},{3,128},{128,129},{129,130},{130,131},{131,256},... | collective-permute-start | bytes 6152 | tf_op jit(solution)/shard_map/ppermute | solution.py:24
  438.7 21.7 %collective-permute-start.22 = (f32[4,1,32]{2,0,1:T(4,128)S(1)}, f32[4,1,32]{2,0,1:T(4,128)S(1)}, u32[]{:S(2)}, u32[]{:S(2)}) collective-permute-start(f32[4,1,32]{2,0,1:T(4,128)S(1)} %get-tuple-element.157), channel_id=1, source_target_pairs={{1,0},{2,1},{3,2},{128,3},{129,128},{130,129},{131,130},{256,131},... | collective-permute-start | bytes 1544 | tf_op jit(solution)/shard_map/ppermute | solution.py:25
  440.6 19.8 %collective-permute-start.23 = (f32[4,1,32]{2,0,1:T(4,128)S(1)}, f32[4,1,32]{2,0,1:T(4,128)S(1)}, u32[]{:S(2)}, u32[]{:S(2)}) collective-permute-start(f32[4,1,32]{2,0,1:T(4,128)S(1)} %get-tuple-element.156), channel_id=1, source_target_pairs={{0,1},{1,2},{2,3},{3,128},{128,129},{129,130},{130,131},{131,256},... | collective-permute-start | bytes 1544 | tf_op jit(solution)/shard_map/ppermute | solution.py:24
  464.8 21.7 %collective-permute-start.26 = (f32[4,1,32]{2,0,1:T(4,128)S(1)}, f32[4,1,32]{2,0,1:T(4,128)S(1)}, u32[]{:S(2)}, u32[]{:S(2)}) collective-permute-start(f32[4,1,32]{2,0,1:T(4,128)S(1)} %get-tuple-element.153), channel_id=1, source_target_pairs={{1,0},{2,1},{3,2},{128,3},{129,128},{130,129},{131,130},{256,131},... | collective-permute-start | bytes 1544 | tf_op jit(solution)/shard_map/ppermute | solution.py:25
  466.7 19.8 %collective-permute-start.27 = (f32[4,1,32]{2,0,1:T(4,128)S(1)}, f32[4,1,32]{2,0,1:T(4,128)S(1)}, u32[]{:S(2)}, u32[]{:S(2)}) collective-permute-start(f32[4,1,32]{2,0,1:T(4,128)S(1)} %get-tuple-element.152), channel_id=1, source_target_pairs={{0,1},{1,2},{2,3},{3,128},{128,129},{129,130},{130,131},{131,256},... | collective-permute-start | bytes 1544 | tf_op jit(solution)/shard_map/ppermute | solution.py:24
  491.0 21.7 %collective-permute-start.30 = (f32[4,1,32]{2,0,1:T(4,128)S(1)}, f32[4,1,32]{2,0,1:T(4,128)S(1)}, u32[]{:S(2)}, u32[]{:S(2)}) collective-permute-start(f32[4,1,32]{2,0,1:T(4,128)S(1)} %get-tuple-element.149), channel_id=1, source_target_pairs={{1,0},{2,1},{3,2},{128,3},{129,128},{130,129},{131,130},{256,131},... | collective-permute-start | bytes 1544 | tf_op jit(solution)/shard_map/ppermute | solution.py:25
  492.9 19.8 %collective-permute-start.31 = (f32[4,1,32]{2,0,1:T(4,128)S(1)}, f32[4,1,32]{2,0,1:T(4,128)S(1)}, u32[]{:S(2)}, u32[]{:S(2)}) collective-permute-start(f32[4,1,32]{2,0,1:T(4,128)S(1)} %get-tuple-element.148), channel_id=1, source_target_pairs={{0,1},{1,2},{2,3},{3,128},{128,129},{129,130},{130,131},{131,256},... | collective-permute-start | bytes 1544 | tf_op jit(solution)/shard_map/ppermute | solution.py:24
  517.4 21.7 %collective-permute-start.34 = (f32[8,1,64]{2,1,0:T(1,128)S(1)}, f32[8,1,64]{2,1,0:T(1,128)S(1)}, u32[]{:S(2)}, u32[]{:S(2)}) collective-permute-start(f32[8,1,64]{2,1,0:T(1,128)S(1)} %get-tuple-element.125), channel_id=1, source_target_pairs={{1,0},{2,1},{3,2},{128,3},{129,128},{130,129},{131,130},{256,131},... | collective-permute-start | bytes 6152 | tf_op jit(solution)/shard_map/ppermute | solution.py:25
  519.3 19.8 %collective-permute-start.35 = (f32[8,1,64]{2,1,0:T(1,128)S(1)}, f32[8,1,64]{2,1,0:T(1,128)S(1)}, u32[]{:S(2)}, u32[]{:S(2)}) collective-permute-start(f32[8,1,64]{2,1,0:T(1,128)S(1)} %get-tuple-element.124), channel_id=1, source_target_pairs={{0,1},{1,2},{2,3},{3,128},{128,129},{129,130},{130,131},{131,256},... | collective-permute-start | bytes 6152 | tf_op jit(solution)/shard_map/ppermute | solution.py:24
  543.6 21.7 %collective-permute-start.38 = (f32[8,1,64]{2,1,0:T(1,128)S(1)}, f32[8,1,64]{2,1,0:T(1,128)S(1)}, u32[]{:S(2)}, u32[]{:S(2)}) collective-permute-start(f32[8,1,64]{2,1,0:T(1,128)S(1)} %get-tuple-element.121), channel_id=1, source_target_pairs={{1,0},{2,1},{3,2},{128,3},{129,128},{130,129},{131,130},{256,131},... | collective-permute-start | bytes 6152 | tf_op jit(solution)/shard_map/ppermute | solution.py:25
  545.5 19.8 %collective-permute-start.39 = (f32[8,1,64]{2,1,0:T(1,128)S(1)}, f32[8,1,64]{2,1,0:T(1,128)S(1)}, u32[]{:S(2)}, u32[]{:S(2)}) collective-permute-start(f32[8,1,64]{2,1,0:T(1,128)S(1)} %get-tuple-element.120), channel_id=1, source_target_pairs={{0,1},{1,2},{2,3},{3,128},{128,129},{129,130},{130,131},{131,256},... | collective-permute-start | bytes 6152 | tf_op jit(solution)/shard_map/ppermute | solution.py:24
  570.3 21.7 %collective-permute-start.42 = (f32[16,1,128]{2,1,0:T(1,128)S(1)}, f32[16,1,128]{2,1,0:T(1,128)S(1)}, u32[]{:S(2)}, u32[]{:S(2)}) collective-permute-start(f32[16,1,128]{2,1,0:T(1,128)S(1)} %get-tuple-element.89), channel_id=1, source_target_pairs={{1,0},{2,1},{3,2},{128,3},{129,128},{130,129},{131,130},{256,131},... | collective-permute-start | bytes 24584 | tf_op jit(solution)/shard_map/ppermute | solution.py:25
  572.2 19.8 %collective-permute-start.43 = (f32[16,1,128]{2,1,0:T(1,128)S(1)}, f32[16,1,128]{2,1,0:T(1,128)S(1)}, u32[]{:S(2)}, u32[]{:S(2)}) collective-permute-start(f32[16,1,128]{2,1,0:T(1,128)S(1)} %get-tuple-element.88), channel_id=1, source_target_pairs={{0,1},{1,2},{2,3},{3,128},{128,129},{129,130},{130,131},{131,256},... | collective-permute-start | bytes 24584 | tf_op jit(solution)/shard_map/ppermute | solution.py:24
  588.6 7.7 collective-permute-start.41
  596.7 21.7 %collective-permute-start.46 = (f32[16,1,128]{2,1,0:T(1,128)S(1)}, f32[16,1,128]{2,1,0:T(1,128)S(1)}, u32[]{:S(2)}, u32[]{:S(2)}) collective-permute-start(f32[16,1,128]{2,1,0:T(1,128)S(1)} %get-tuple-element.85), channel_id=1, source_target_pairs={{1,0},{2,1},{3,2},{128,3},{129,128},{130,129},{131,130},{256,131},... | collective-permute-start | bytes 24584 | tf_op jit(solution)/shard_map/ppermute | solution.py:25
  598.6 19.8 %collective-permute-start.47 = (f32[16,1,128]{2,1,0:T(1,128)S(1)}, f32[16,1,128]{2,1,0:T(1,128)S(1)}, u32[]{:S(2)}, u32[]{:S(2)}) collective-permute-start(f32[16,1,128]{2,1,0:T(1,128)S(1)} %get-tuple-element.84), channel_id=1, source_target_pairs={{0,1},{1,2},{2,3},{3,128},{128,129},{129,130},{130,131},{131,256},... | collective-permute-start | bytes 24584 | tf_op jit(solution)/shard_map/ppermute | solution.py:24
  615.0 7.7 collective-permute-start.45
  623.0 21.7 %collective-permute-start.50 = (f32[16,1,128]{2,1,0:T(1,128)S(1)}, f32[16,1,128]{2,1,0:T(1,128)S(1)}, u32[]{:S(2)}, u32[]{:S(2)}) collective-permute-start(f32[16,1,128]{2,1,0:T(1,128)S(1)} %get-tuple-element.81), channel_id=1, source_target_pairs={{1,0},{2,1},{3,2},{128,3},{129,128},{130,129},{131,130},{256,131},... | collective-permute-start | bytes 24584 | tf_op jit(solution)/shard_map/ppermute | solution.py:25
  624.9 19.8 %collective-permute-start.51 = (f32[16,1,128]{2,1,0:T(1,128)S(1)}, f32[16,1,128]{2,1,0:T(1,128)S(1)}, u32[]{:S(2)}, u32[]{:S(2)}) collective-permute-start(f32[16,1,128]{2,1,0:T(1,128)S(1)} %get-tuple-element.80), channel_id=1, source_target_pairs={{0,1},{1,2},{2,3},{3,128},{128,129},{129,130},{130,131},{131,256},... | collective-permute-start | bytes 24584 | tf_op jit(solution)/shard_map/ppermute | solution.py:24
  649.4 41.3 %collective-permute-start.54 = (f32[16,1,128]{2,1,0:T(1,128)S(1)}, f32[16,1,128]{2,1,0:T(1,128)S(1)}, u32[]{:S(2)}, u32[]{:S(2)}) collective-permute-start(f32[16,1,128]{2,1,0:T(1,128)S(1)} %get-tuple-element.77), channel_id=1, source_target_pairs={{1,0},{2,1},{3,2},{128,3},{129,128},{130,129},{131,130},{256,131},... | collective-permute-start | bytes 24584 | tf_op jit(solution)/shard_map/ppermute | solution.py:25
  651.3 39.4 %collective-permute-start.55 = (f32[16,1,128]{2,1,0:T(1,128)S(1)}, f32[16,1,128]{2,1,0:T(1,128)S(1)}, u32[]{:S(2)}, u32[]{:S(2)}) collective-permute-start(f32[16,1,128]{2,1,0:T(1,128)S(1)} %get-tuple-element.76), channel_id=1, source_target_pairs={{0,1},{1,2},{2,3},{3,128},{128,129},{129,130},{130,131},{131,256},... | collective-permute-start | bytes 24584 | tf_op jit(solution)/shard_map/ppermute | solution.py:24
  665.8 24.9 %collective-permute-start.52 = (f32[1,8,128]{2,1,0:T(8,128)S(1)}, f32[1,8,128]{2,1,0:T(8,128)S(1)}, u32[]{:S(2)}, u32[]{:S(2)}) collective-permute-start(f32[1,8,128]{2,1,0:T(8,128)S(1)} %get-tuple-element.75), channel_id=1, source_target_pairs={{4,0},{8,4},{12,8},{16,12},{20,16},{24,20},{28,24},{32,28},{36,32}... | collective-permute-start | bytes 12296 | tf_op jit(solution)/shard_map/ppermute | solution.py:25
  667.7 23.0 %collective-permute-start.53 = (f32[1,8,128]{2,1,0:T(8,128)S(1)}, f32[1,8,128]{2,1,0:T(8,128)S(1)}, u32[]{:S(2)}, u32[]{:S(2)}) collective-permute-start(f32[1,8,128]{2,1,0:T(8,128)S(1)} %get-tuple-element.74), channel_id=1, source_target_pairs={{0,4},{4,8},{8,12},{12,16},{16,20},{20,24},{24,28},{28,32},{32,36}... | collective-permute-start | bytes 12296 | tf_op jit(solution)/shard_map/ppermute | solution.py:24
  686.4 156.6 %all-to-all-start.4 = ((f32[16,1,16384]{2,1,0:T(1,128)}), f32[16,1,16384]{2,1,0:T(1,128)S(1)}, u32[]{:S(2)}, u32[]{:S(2)}) async-start(f32[16,1,16384]{2,1,0:T(1,128)} %reshape.363), calls=%async_computation.4 | async-start | bytes 2097152 | tf_op jit(solution)/shard_map/all_to_all | solution.py:158
  691.1 23.6 %collective-permute-start.58 = (f32[16,1,128]{2,1,0:T(1,128)S(1)}, f32[16,1,128]{2,1,0:T(1,128)S(1)}, u32[]{:S(2)}, u32[]{:S(2)}) collective-permute-start(f32[16,1,128]{2,1,0:T(1,128)S(1)} %get-tuple-element.73), channel_id=1, source_target_pairs={{1,0},{2,1},{3,2},{128,3},{129,128},{130,129},{131,130},{256,131},... | collective-permute-start | bytes 24584 | tf_op jit(solution)/shard_map/ppermute | solution.py:25
  693.6 21.1 %collective-permute-start.59 = (f32[16,1,128]{2,1,0:T(1,128)S(1)}, f32[16,1,128]{2,1,0:T(1,128)S(1)}, u32[]{:S(2)}, u32[]{:S(2)}) collective-permute-start(f32[16,1,128]{2,1,0:T(1,128)S(1)} %get-tuple-element.72), channel_id=1, source_target_pairs={{0,1},{1,2},{2,3},{3,128},{128,129},{129,130},{130,131},{131,256},... | collective-permute-start | bytes 24584 | tf_op jit(solution)/shard_map/ppermute | solution.py:24
  712.7 8.1 collective-permute-start.57
  729.2 21.7 %collective-permute-start.62 = (f32[8,1,64]{2,1,0:T(1,128)S(1)}, f32[8,1,64]{2,1,0:T(1,128)S(1)}, u32[]{:S(2)}, u32[]{:S(2)}) collective-permute-start(f32[8,1,64]{2,1,0:T(1,128)S(1)} %get-tuple-element.117), channel_id=1, source_target_pairs={{1,0},{2,1},{3,2},{128,3},{129,128},{130,129},{131,130},{256,131},... | collective-permute-start | bytes 6152 | tf_op jit(solution)/shard_map/ppermute | solution.py:25
  731.1 19.8 %collective-permute-start.63 = (f32[8,1,64]{2,1,0:T(1,128)S(1)}, f32[8,1,64]{2,1,0:T(1,128)S(1)}, u32[]{:S(2)}, u32[]{:S(2)}) collective-permute-start(f32[8,1,64]{2,1,0:T(1,128)S(1)} %get-tuple-element.116), channel_id=1, source_target_pairs={{0,1},{1,2},{2,3},{3,128},{128,129},{129,130},{130,131},{131,256},... | collective-permute-start | bytes 6152 | tf_op jit(solution)/shard_map/ppermute | solution.py:24
  747.6 14.0 %collective-permute-start.61 = (f32[1,4,64]{2,1,0:T(4,128)S(1)}, f32[1,4,64]{2,1,0:T(4,128)S(1)}, u32[]{:S(2)}, u32[]{:S(2)}) collective-permute-start(f32[1,4,64]{2,1,0:T(4,128)S(1)} %get-tuple-element.114), channel_id=1, source_target_pairs={{0,4},{4,8},{8,12},{12,16},{16,20},{20,24},{24,28},{28,32},{32,36}... | collective-permute-start | bytes 3080 | tf_op jit(solution)/shard_map/ppermute | solution.py:24
  761.8 22.4 %collective-permute-start.66 = (f32[8,1,64]{2,1,0:T(1,128)S(1)}, f32[8,1,64]{2,1,0:T(1,128)S(1)}, u32[]{:S(2)}, u32[]{:S(2)}) collective-permute-start(f32[8,1,64]{2,1,0:T(1,128)S(1)} %get-tuple-element.113), channel_id=1, source_target_pairs={{1,0},{2,1},{3,2},{128,3},{129,128},{130,129},{131,130},{256,131},... | collective-permute-start | bytes 6152 | tf_op jit(solution)/shard_map/ppermute | solution.py:25
  763.7 20.5 %collective-permute-start.67 = (f32[8,1,64]{2,1,0:T(1,128)S(1)}, f32[8,1,64]{2,1,0:T(1,128)S(1)}, u32[]{:S(2)}, u32[]{:S(2)}) collective-permute-start(f32[8,1,64]{2,1,0:T(1,128)S(1)} %get-tuple-element.112), channel_id=1, source_target_pairs={{0,1},{1,2},{2,3},{3,128},{128,129},{129,130},{130,131},{131,256},... | collective-permute-start | bytes 6152 | tf_op jit(solution)/shard_map/ppermute | solution.py:24
  790.8 21.7 %collective-permute-start.70 = (f32[4,1,32]{2,0,1:T(4,128)S(1)}, f32[4,1,32]{2,0,1:T(4,128)S(1)}, u32[]{:S(2)}, u32[]{:S(2)}) collective-permute-start(f32[4,1,32]{2,0,1:T(4,128)S(1)} %get-tuple-element.145), channel_id=1, source_target_pairs={{1,0},{2,1},{3,2},{128,3},{129,128},{130,129},{131,130},{256,131},... | collective-permute-start | bytes 1544 | tf_op jit(solution)/shard_map/ppermute | solution.py:25
  792.7 19.8 %collective-permute-start.71 = (f32[4,1,32]{2,0,1:T(4,128)S(1)}, f32[4,1,32]{2,0,1:T(4,128)S(1)}, u32[]{:S(2)}, u32[]{:S(2)}) collective-permute-start(f32[4,1,32]{2,0,1:T(4,128)S(1)} %get-tuple-element.144), channel_id=1, source_target_pairs={{0,1},{1,2},{2,3},{3,128},{128,129},{129,130},{130,131},{131,256},... | collective-permute-start | bytes 1544 | tf_op jit(solution)/shard_map/ppermute | solution.py:24
  816.9 21.7 %collective-permute-start.74 = (f32[4,1,32]{2,0,1:T(4,128)S(1)}, f32[4,1,32]{2,0,1:T(4,128)S(1)}, u32[]{:S(2)}, u32[]{:S(2)}) collective-permute-start(f32[4,1,32]{2,0,1:T(4,128)S(1)} %get-tuple-element.141), channel_id=1, source_target_pairs={{1,0},{2,1},{3,2},{128,3},{129,128},{130,129},{131,130},{256,131},... | collective-permute-start | bytes 1544 | tf_op jit(solution)/shard_map/ppermute | solution.py:25
  818.9 19.8 %collective-permute-start.75 = (f32[4,1,32]{2,0,1:T(4,128)S(1)}, f32[4,1,32]{2,0,1:T(4,128)S(1)}, u32[]{:S(2)}, u32[]{:S(2)}) collective-permute-start(f32[4,1,32]{2,0,1:T(4,128)S(1)} %get-tuple-element.140), channel_id=1, source_target_pairs={{0,1},{1,2},{2,3},{3,128},{128,129},{129,130},{130,131},{131,256},... | collective-permute-start | bytes 1544 | tf_op jit(solution)/shard_map/ppermute | solution.py:24
  874.5 143.6 %all-to-all-start.5 = ((f32[32,1,8192]{2,1,0:T(1,128)}), f32[32,1,8192]{2,1,0:T(1,128)S(1)}, u32[]{:S(2)}, u32[]{:S(2)}) async-start(f32[32,1,8192]{2,1,0:T(1,128)} %reshape.365), calls=%async_computation.5 | async-start | bytes 2097152 | tf_op jit(solution)/shard_map/all_to_all | solution.py:164
  883.0 22.6 %collective-permute-start.78 = (f32[4,1,32]{2,0,1:T(4,128)S(1)}, f32[4,1,32]{2,0,1:T(4,128)S(1)}, u32[]{:S(2)}, u32[]{:S(2)}) collective-permute-start(f32[4,1,32]{2,0,1:T(4,128)S(1)} %get-tuple-element.137), channel_id=1, source_target_pairs={{1,0},{2,1},{3,2},{128,3},{129,128},{130,129},{131,130},{256,131},... | collective-permute-start | bytes 1544 | tf_op jit(solution)/shard_map/ppermute | solution.py:25
  884.9 20.8 %collective-permute-start.79 = (f32[4,1,32]{2,0,1:T(4,128)S(1)}, f32[4,1,32]{2,0,1:T(4,128)S(1)}, u32[]{:S(2)}, u32[]{:S(2)}) collective-permute-start(f32[4,1,32]{2,0,1:T(4,128)S(1)} %get-tuple-element.136), channel_id=1, source_target_pairs={{0,1},{1,2},{2,3},{3,128},{128,129},{129,130},{130,131},{131,256},... | collective-permute-start | bytes 1544 | tf_op jit(solution)/shard_map/ppermute | solution.py:24
  911.8 21.7 %collective-permute-start.82 = (f32[8,1,64]{2,1,0:T(1,128)S(1)}, f32[8,1,64]{2,1,0:T(1,128)S(1)}, u32[]{:S(2)}, u32[]{:S(2)}) collective-permute-start(f32[8,1,64]{2,1,0:T(1,128)S(1)} %get-tuple-element.109), channel_id=1, source_target_pairs={{1,0},{2,1},{3,2},{128,3},{129,128},{130,129},{131,130},{256,131},... | collective-permute-start | bytes 6152 | tf_op jit(solution)/shard_map/ppermute | solution.py:25
  913.7 19.8 %collective-permute-start.83 = (f32[8,1,64]{2,1,0:T(1,128)S(1)}, f32[8,1,64]{2,1,0:T(1,128)S(1)}, u32[]{:S(2)}, u32[]{:S(2)}) collective-permute-start(f32[8,1,64]{2,1,0:T(1,128)S(1)} %get-tuple-element.108), channel_id=1, source_target_pairs={{0,1},{1,2},{2,3},{3,128},{128,129},{129,130},{130,131},{131,256},... | collective-permute-start | bytes 6152 | tf_op jit(solution)/shard_map/ppermute | solution.py:24
  938.0 21.7 %collective-permute-start.86 = (f32[8,1,64]{2,1,0:T(1,128)S(1)}, f32[8,1,64]{2,1,0:T(1,128)S(1)}, u32[]{:S(2)}, u32[]{:S(2)}) collective-permute-start(f32[8,1,64]{2,1,0:T(1,128)S(1)} %get-tuple-element.105), channel_id=1, source_target_pairs={{1,0},{2,1},{3,2},{128,3},{129,128},{130,129},{131,130},{256,131},... | collective-permute-start | bytes 6152 | tf_op jit(solution)/shard_map/ppermute | solution.py:25
  939.9 19.8 %collective-permute-start.87 = (f32[8,1,64]{2,1,0:T(1,128)S(1)}, f32[8,1,64]{2,1,0:T(1,128)S(1)}, u32[]{:S(2)}, u32[]{:S(2)}) collective-permute-start(f32[8,1,64]{2,1,0:T(1,128)S(1)} %get-tuple-element.104), channel_id=1, source_target_pairs={{0,1},{1,2},{2,3},{3,128},{128,129},{129,130},{130,131},{131,256},... | collective-permute-start | bytes 6152 | tf_op jit(solution)/shard_map/ppermute | solution.py:24
  964.7 21.7 %collective-permute-start.90 = (f32[16,1,128]{2,1,0:T(1,128)S(1)}, f32[16,1,128]{2,1,0:T(1,128)S(1)}, u32[]{:S(2)}, u32[]{:S(2)}) collective-permute-start(f32[16,1,128]{2,1,0:T(1,128)S(1)} %get-tuple-element.69), channel_id=1, source_target_pairs={{1,0},{2,1},{3,2},{128,3},{129,128},{130,129},{131,130},{256,131},... | collective-permute-start | bytes 24584 | tf_op jit(solution)/shard_map/ppermute | solution.py:25
  966.7 19.8 %collective-permute-start.91 = (f32[16,1,128]{2,1,0:T(1,128)S(1)}, f32[16,1,128]{2,1,0:T(1,128)S(1)}, u32[]{:S(2)}, u32[]{:S(2)}) collective-permute-start(f32[16,1,128]{2,1,0:T(1,128)S(1)} %get-tuple-element.68), channel_id=1, source_target_pairs={{0,1},{1,2},{2,3},{3,128},{128,129},{129,130},{130,131},{131,256},... | collective-permute-start | bytes 24584 | tf_op jit(solution)/shard_map/ppermute | solution.py:24
  991.1 21.7 %collective-permute-start.94 = (f32[16,1,128]{2,1,0:T(1,128)S(1)}, f32[16,1,128]{2,1,0:T(1,128)S(1)}, u32[]{:S(2)}, u32[]{:S(2)}) collective-permute-start(f32[16,1,128]{2,1,0:T(1,128)S(1)} %get-tuple-element.65), channel_id=1, source_target_pairs={{1,0},{2,1},{3,2},{128,3},{129,128},{130,129},{131,130},{256,131},... | collective-permute-start | bytes 24584 | tf_op jit(solution)/shard_map/ppermute | solution.py:25
  993.0 19.8 %collective-permute-start.95 = (f32[16,1,128]{2,1,0:T(1,128)S(1)}, f32[16,1,128]{2,1,0:T(1,128)S(1)}, u32[]{:S(2)}, u32[]{:S(2)}) collective-permute-start(f32[16,1,128]{2,1,0:T(1,128)S(1)} %get-tuple-element.64), channel_id=1, source_target_pairs={{0,1},{1,2},{2,3},{3,128},{128,129},{129,130},{130,131},{131,256},... | collective-permute-start | bytes 24584 | tf_op jit(solution)/shard_map/ppermute | solution.py:24
  (44 other events, 369.3 us)
where the time goes:
time: 1060 us; the launch traced here: 1050 us
  starting transfers between devices  608 us (57%)
  waiting for transfers between devices  200 us (19%)
  local copies, waits for them, and re-layouts  120 us (11%)
  matrix products  61.1 us (6%)
  other arithmetic  32.9 us (3%)
  blocking collectives  18.9 us (2%)
    ppermute x48, starting transfers between devices, extended(): lax.ppermute(last, axis, up)  420 us
    ppermute x48, starting transfers between devices, extended(): lax.ppermute(initial, axis, [(b, a) for a, b in up])  111 us
    ppermute x48, waiting for transfers between devices, extended(): lax.ppermute(last, axis, up)  105 us
    all_to_all x1, waiting for transfers between devices, local(): lax.all_to_all(dense, ('group', 'gy'), split_axis=0, concat_axis=1, tiled...  50.5 us
    unnamed x26, local copies, waits for them, and re-layouts  37.8 us
    all_to_all x1, waiting for transfers between devices, local(): lax.all_to_all(dense, 'gx', split_axis=2, concat_axis=0, tiled=True)  37.1 us
    dot_general x4, matrix products, last_axis(): return jnp.einsum('abj,kj->abk', block, table, precision=HIGH)  26.1 us
  transfers between devices with their start and end apart: 103, of which 27 were waited for; matrix products, arithmetic and copies ran while one was open for 9% of the time, Pallas kernels for 0%

commit v1 on v0

--- a/solution.py
+++ b/solution.py
@@ -135,7 +135,10 @@
     dense = last_axis(parent_mass, full)
     light = last_axis(rest, z_table)
     dense, light = (
-        lax.all_to_all(dense, "gx", split_axis=2, concat_axis=0, tiled=True),
+        jnp.concatenate(
+            lax.all_to_all(jnp.stack(jnp.split(dense, lax.axis_size("gx"), axis=2)), "gx", 0, 0),
+            axis=0,
+        ),
         lax.all_to_all(light, "gx", split_axis=2, concat_axis=0, tiled=True),
     )
     dense = first_axis(dense, full)

time: 1060 us -> 1090 us (1.028)
  local copies, waits for them, and re-layouts: 120 us -> 151 us
  starting transfers between devices: 608 us -> 597 us
    unnamed x26 -> x55, local copies, waits for them, and re-layouts: 37.8 us -> 63.6 us
    another operation x2 -> x5, local copies, waits for them, and re-layouts: 0.59 us -> 16 us  [the longest x1 7.77 us: first_axis(): product = jnp.dot(table, block.reshape(block.shape[0], -1), precision=HIGH)]
  transfers between devices with their start and end apart: 103 -> 103, of which waited for: 27 -> 29; matrix products, arithmetic and copies ran while one was open for 9% -> 11% of each run, Pallas kernels for 0% -> 0%
where the time goes in v1:
time: 1090 us; the launch traced here: 1070 us
  starting transfers between devices  597 us (55%)
  waiting for transfers between devices  209 us (19%)
  local copies, waits for them, and re-layouts  151 us (14%)
  matrix products  61.1 us (6%)
  other arithmetic  32.9 us (3%)
  blocking collectives  18.9 us (2%)
    ppermute x48, starting transfers between devices, extended(): lax.ppermute(last, axis, up)  413 us
    ppermute x48, starting transfers between devices, extended(): lax.ppermute(initial, axis, [(b, a) for a, b in up])  110 us
    ppermute x48, waiting for transfers between devices, extended(): lax.ppermute(last, axis, up)  106 us
    unnamed x55, local copies, waits for them, and re-layouts  63.6 us
    all_to_all x1, waiting for transfers between devices, local(): lax.all_to_all(dense, ('group', 'gy'), split_axis=0, concat_axis=1, tiled...  50.6 us
    all_to_all x1, waiting for transfers between devices, local(): lax.all_to_all(jnp.stack(jnp.split(dense, lax.axis_size('gx'), axis=2)),...  37.3 us
    dot_general x4, matrix products, last_axis(): return jnp.einsum('abj,kj->abk', block, table, precision=HIGH)  26.1 us
  transfers between devices with their start and end apart: 103, of which 29 were waited for; matrix products, arithmetic and copies ran while one was open for 11% of the time, Pallas kernels for 0%

profile of v1, /device:TPU:135, one launch (start us, length us, event | category | flops | bytes accessed | tf_op | source)
XLA Modules:
  0.0 1073.1 jit_solution(9331620526960282947)
XLA Ops:
  2.7 6.3 reshape.321
  14.6 13.5 %all-to-all-start.2 = ((f32[32,1,512]{2,1,0:T(1,128)}), f32[32,1,512]{2,1,0:T(1,128)S(1)}, u32[]{:S(2)}, u32[]{:S(2)}) async-start(f32[32,1,512]{2,1,0:T(1,128)} %reshape.354), calls=%async_computation.2 | async-start | bytes 131072 | tf_op jit(solution)/shard_map/all_to_all | solution.py:142
  28.1 6.7 convolution_bitcast_fusion.1
  61.4 6.8 copy.581
  68.2 4.7 reshape.350
  72.9 12.0 %all-to-all-start = ((f32[32,1,8192]{2,1,0:T(1,128)}), f32[32,1,8192]{2,1,0:T(1,128)S(1)}, u32[]{:S(2)}, u32[]{:S(2)}) async-start(f32[32,1,8192]{2,1,0:T(1,128)} %reshape.350), calls=%async_computation | async-start | bytes 2097152 | tf_op jit(solution)/shard_map/all_to_all | solution.py:139
  93.9 37.3 %all-to-all-done = f32[32,1,8192]{2,1,0:T(1,128)S(1)} async-done(((f32[32,1,8192]{2,1,0:T(1,128)}), f32[32,1,8192]{2,1,0:T(1,128)S(1)}, u32[]{:S(2)}, u32[]{:S(2)}) %all-to-all-start) | async-done | bytes 1048608 | tf_op jit(solution)/shard_map/all_to_all | solution.py:139
  131.2 11.4 %all-to-all-start.3 = ((f32[16,1,2048]{2,1,0:T(1,128)}), f32[16,1,2048]{2,1,0:T(1,128)S(1)}, u32[]{:S(2)}, u32[]{:S(2)}) async-start(f32[16,1,2048]{2,1,0:T(1,128)} %reshape.356), calls=%async_computation.3 | async-start | bytes 262144 | tf_op jit(solution)/shard_map/all_to_all | solution.py:148
  148.6 7.0 copy.582
  155.6 7.8 reshape_reshape.3
  163.8 6.4 fusion.15
  173.8 4.7 reshape.352
  178.5 14.7 %all-to-all-start.1 = ((f32[16,1,16384]{2,1,0:T(1,128)}), f32[16,1,16384]{2,1,0:T(1,128)S(1)}, u32[]{:S(2)}, u32[]{:S(2)}) async-start(f32[16,1,16384]{2,1,0:T(1,128)} %reshape.352), calls=%async_computation.1 | async-start | bytes 2097152 | tf_op jit(solution)/shard_map/all_to_all | solution.py:147
  197.0 50.6 %all-to-all-done.1 = f32[16,1,16384]{2,1,0:T(1,128)S(1)} async-done(((f32[16,1,16384]{2,1,0:T(1,128)}), f32[16,1,16384]{2,1,0:T(1,128)S(1)}, u32[]{:S(2)}, u32[]{:S(2)}) %all-to-all-start.1) | async-done | bytes 1048608 | tf_op jit(solution)/shard_map/all_to_all | solution.py:147
  253.6 6.7 copy.646
  263.9 7.1 fusion.13
  274.9 18.9 %all_to_all.122 = f32[16,1,2048]{2,1,0:T(1,128)S(1)} all-to-all(f32[16,1,2048]{2,1,0:T(1,128)S(1)} %reshape.362), channel_id=1, replica_groups=mesh['group'=4,'gx'=32,'gy'=4] {'group','gy'}, dimensions={0} | all-to-all | bytes 262144 | tf_op jit(solution)/shard_map/all_to_all | solution.py:162
  299.3 12.1 %all-to-all-start.7 = ((f32[32,1,512]{2,1,0:T(1,128)}), f32[32,1,512]{2,1,0:T(1,128)S(1)}, u32[]{:S(2)}, u32[]{:S(2)}) async-start(f32[32,1,512]{2,1,0:T(1,128)} %reshape.364), calls=%async_computation.7 | async-start | bytes 131072 | tf_op jit(solution)/shard_map/all_to_all | solution.py:168
  312.1 6.4 all-to-all-done.7
  324.0 6.5 collective-permute-start
  332.5 6.4 collective-permute-start.2
  339.7 6.7 collective-permute-done.3
  350.3 14.5 %collective-permute-start.7 = (f32[16,1,128]{2,1,0:T(1,128)S(1)}, f32[16,1,128]{2,1,0:T(1,128)S(1)}, u32[]{:S(2)}, u32[]{:S(2)}) collective-permute-start(f32[16,1,128]{2,1,0:T(1,128)S(1)} %get-tuple-element.96), channel_id=1, source_target_pairs={{0,1},{1,2},{2,3},{3,128},{128,129},{129,130},{130,131},{131,256},... | collective-permute-start | bytes 24584 | tf_op jit(solution)/shard_map/ppermute | solution.py:24
  364.8 6.4 collective-permute-start.4
  373.2 5.7 collective-permute-done.5
  381.2 14.5 %collective-permute-start.11 = (f32[16,1,128]{2,1,0:T(1,128)S(1)}, f32[16,1,128]{2,1,0:T(1,128)S(1)}, u32[]{:S(2)}, u32[]{:S(2)}) collective-permute-start(f32[16,1,128]{2,1,0:T(1,128)S(1)} %get-tuple-element.92), channel_id=1, source_target_pairs={{0,1},{1,2},{2,3},{3,128},{128,129},{129,130},{130,131},{131,256},... | collective-permute-start | bytes 24584 | tf_op jit(solution)/shard_map/ppermute | solution.py:24
  405.8 5.5 reshape.330
  415.8 14.5 %collective-permute-start.15 = (f32[8,1,64]{2,1,0:T(1,128)S(1)}, f32[8,1,64]{2,1,0:T(1,128)S(1)}, u32[]{:S(2)}, u32[]{:S(2)}) collective-permute-start(f32[8,1,64]{2,1,0:T(1,128)S(1)} %get-tuple-element.132), channel_id=1, source_target_pairs={{0,1},{1,2},{2,3},{3,128},{128,129},{129,130},{130,131},{131,256},... | collective-permute-start | bytes 6152 | tf_op jit(solution)/shard_map/ppermute | solution.py:24
  442.0 14.5 %collective-permute-start.19 = (f32[8,1,64]{2,1,0:T(1,128)S(1)}, f32[8,1,64]{2,1,0:T(1,128)S(1)}, u32[]{:S(2)}, u32[]{:S(2)}) collective-permute-start(f32[8,1,64]{2,1,0:T(1,128)S(1)} %get-tuple-element.128), channel_id=1, source_target_pairs={{0,1},{1,2},{2,3},{3,128},{128,129},{129,130},{130,131},{131,256},... | collective-permute-start | bytes 6152 | tf_op jit(solution)/shard_map/ppermute | solution.py:24
  468.9 14.5 %collective-permute-start.23 = (f32[4,1,32]{2,0,1:T(4,128)S(1)}, f32[4,1,32]{2,0,1:T(4,128)S(1)}, u32[]{:S(2)}, u32[]{:S(2)}) collective-permute-start(f32[4,1,32]{2,0,1:T(4,128)S(1)} %get-tuple-element.156), channel_id=1, source_target_pairs={{0,1},{1,2},{2,3},{3,128},{128,129},{129,130},{130,131},{131,256},... | collective-permute-start | bytes 1544 | tf_op jit(solution)/shard_map/ppermute | solution.py:24
  495.1 14.5 %collective-permute-start.27 = (f32[4,1,32]{2,0,1:T(4,128)S(1)}, f32[4,1,32]{2,0,1:T(4,128)S(1)}, u32[]{:S(2)}, u32[]{:S(2)}) collective-permute-start(f32[4,1,32]{2,0,1:T(4,128)S(1)} %get-tuple-element.152), channel_id=1, source_target_pairs={{0,1},{1,2},{2,3},{3,128},{128,129},{129,130},{130,131},{131,256},... | collective-permute-start | bytes 1544 | tf_op jit(solution)/shard_map/ppermute | solution.py:24
  521.2 14.5 %collective-permute-start.31 = (f32[4,1,32]{2,0,1:T(4,128)S(1)}, f32[4,1,32]{2,0,1:T(4,128)S(1)}, u32[]{:S(2)}, u32[]{:S(2)}) collective-permute-start(f32[4,1,32]{2,0,1:T(4,128)S(1)} %get-tuple-element.148), channel_id=1, source_target_pairs={{0,1},{1,2},{2,3},{3,128},{128,129},{129,130},{130,131},{131,256},... | collective-permute-start | bytes 1544 | tf_op jit(solution)/shard_map/ppermute | solution.py:24
  547.6 14.5 %collective-permute-start.35 = (f32[8,1,64]{2,1,0:T(1,128)S(1)}, f32[8,1,64]{2,1,0:T(1,128)S(1)}, u32[]{:S(2)}, u32[]{:S(2)}) collective-permute-start(f32[8,1,64]{2,1,0:T(1,128)S(1)} %get-tuple-element.124), channel_id=1, source_target_pairs={{0,1},{1,2},{2,3},{3,128},{128,129},{129,130},{130,131},{131,256},... | collective-permute-start | bytes 6152 | tf_op jit(solution)/shard_map/ppermute | solution.py:24
  573.8 14.5 %collective-permute-start.39 = (f32[8,1,64]{2,1,0:T(1,128)S(1)}, f32[8,1,64]{2,1,0:T(1,128)S(1)}, u32[]{:S(2)}, u32[]{:S(2)}) collective-permute-start(f32[8,1,64]{2,1,0:T(1,128)S(1)} %get-tuple-element.120), channel_id=1, source_target_pairs={{0,1},{1,2},{2,3},{3,128},{128,129},{129,130},{130,131},{131,256},... | collective-permute-start | bytes 6152 | tf_op jit(solution)/shard_map/ppermute | solution.py:24
  600.5 14.5 %collective-permute-start.43 = (f32[16,1,128]{2,1,0:T(1,128)S(1)}, f32[16,1,128]{2,1,0:T(1,128)S(1)}, u32[]{:S(2)}, u32[]{:S(2)}) collective-permute-start(f32[16,1,128]{2,1,0:T(1,128)S(1)} %get-tuple-element.88), channel_id=1, source_target_pairs={{0,1},{1,2},{2,3},{3,128},{128,129},{129,130},{130,131},{131,256},... | collective-permute-start | bytes 24584 | tf_op jit(solution)/shard_map/ppermute | solution.py:24
  626.9 14.5 %collective-permute-start.47 = (f32[16,1,128]{2,1,0:T(1,128)S(1)}, f32[16,1,128]{2,1,0:T(1,128)S(1)}, u32[]{:S(2)}, u32[]{:S(2)}) collective-permute-start(f32[16,1,128]{2,1,0:T(1,128)S(1)} %get-tuple-element.84), channel_id=1, source_target_pairs={{0,1},{1,2},{2,3},{3,128},{128,129},{129,130},{130,131},{131,256},... | collective-permute-start | bytes 24584 | tf_op jit(solution)/shard_map/ppermute | solution.py:24
  653.3 14.5 %collective-permute-start.51 = (f32[16,1,128]{2,1,0:T(1,128)S(1)}, f32[16,1,128]{2,1,0:T(1,128)S(1)}, u32[]{:S(2)}, u32[]{:S(2)}) collective-permute-start(f32[16,1,128]{2,1,0:T(1,128)S(1)} %get-tuple-element.80), channel_id=1, source_target_pairs={{0,1},{1,2},{2,3},{3,128},{128,129},{129,130},{130,131},{131,256},... | collective-permute-start | bytes 24584 | tf_op jit(solution)/shard_map/ppermute | solution.py:24
  679.6 14.5 %collective-permute-start.55 = (f32[16,1,128]{2,1,0:T(1,128)S(1)}, f32[16,1,128]{2,1,0:T(1,128)S(1)}, u32[]{:S(2)}, u32[]{:S(2)}) collective-permute-start(f32[16,1,128]{2,1,0:T(1,128)S(1)} %get-tuple-element.76), channel_id=1, source_target_pairs={{0,1},{1,2},{2,3},{3,128},{128,129},{129,130},{130,131},{131,256},... | collective-permute-start | bytes 24584 | tf_op jit(solution)/shard_map/ppermute | solution.py:24
  699.6 6.7 convolution_bitcast_fusion
  710.0 4.7 reshape.358
  714.7 4.2 all-to-all-start.4
  721.9 13.9 %collective-permute-start.59 = (f32[16,1,128]{2,1,0:T(1,128)S(1)}, f32[16,1,128]{2,1,0:T(1,128)S(1)}, u32[]{:S(2)}, u32[]{:S(2)}) collective-permute-start(f32[16,1,128]{2,1,0:T(1,128)S(1)} %get-tuple-element.72), channel_id=1, source_target_pairs={{0,1},{1,2},{2,3},{3,128},{128,129},{129,130},{130,131},{131,256},... | collective-permute-start | bytes 24584 | tf_op jit(solution)/shard_map/ppermute | solution.py:24
  735.8 5.2 collective-permute-start.56
  743.5 5.6 collective-permute-done.57
  749.4 5.5 reshape.338
  759.5 14.5 %collective-permute-start.63 = (f32[8,1,64]{2,1,0:T(1,128)S(1)}, f32[8,1,64]{2,1,0:T(1,128)S(1)}, u32[]{:S(2)}, u32[]{:S(2)}) collective-permute-start(f32[8,1,64]{2,1,0:T(1,128)S(1)} %get-tuple-element.116), channel_id=1, source_target_pairs={{0,1},{1,2},{2,3},{3,128},{128,129},{129,130},{130,131},{131,256},... | collective-permute-start | bytes 6152 | tf_op jit(solution)/shard_map/ppermute | solution.py:24
  779.3 11.7 %collective-permute-done.61 = f32[1,4,64]{2,1,0:T(4,128)S(1)} collective-permute-done((f32[1,4,64]{2,1,0:T(4,128)S(1)}, f32[1,4,64]{2,1,0:T(4,128)S(1)}, u32[]{:S(2)}, u32[]{:S(2)}) %collective-permute-start.61) | collective-permute-done | bytes 1056 | tf_op jit(solution)/shard_map/ppermute | solution.py:24
  793.2 14.5 %collective-permute-start.67 = (f32[8,1,64]{2,1,0:T(1,128)S(1)}, f32[8,1,64]{2,1,0:T(1,128)S(1)}, u32[]{:S(2)}, u32[]{:S(2)}) collective-permute-start(f32[8,1,64]{2,1,0:T(1,128)S(1)} %get-tuple-element.112), channel_id=1, source_target_pairs={{0,1},{1,2},{2,3},{3,128},{128,129},{129,130},{130,131},{131,256},... | collective-permute-start | bytes 6152 | tf_op jit(solution)/shard_map/ppermute | solution.py:24
  813.7 5.7 collective-permute-done.65
  822.1 14.5 %collective-permute-start.71 = (f32[4,1,32]{2,0,1:T(4,128)S(1)}, f32[4,1,32]{2,0,1:T(4,128)S(1)}, u32[]{:S(2)}, u32[]{:S(2)}) collective-permute-start(f32[4,1,32]{2,0,1:T(4,128)S(1)} %get-tuple-element.144), channel_id=1, source_target_pairs={{0,1},{1,2},{2,3},{3,128},{128,129},{129,130},{130,131},{131,256},... | collective-permute-start | bytes 1544 | tf_op jit(solution)/shard_map/ppermute | solution.py:24
  848.3 14.5 %collective-permute-start.75 = (f32[4,1,32]{2,0,1:T(4,128)S(1)}, f32[4,1,32]{2,0,1:T(4,128)S(1)}, u32[]{:S(2)}, u32[]{:S(2)}) collective-permute-start(f32[4,1,32]{2,0,1:T(4,128)S(1)} %get-tuple-element.140), channel_id=1, source_target_pairs={{0,1},{1,2},{2,3},{3,128},{128,129},{129,130},{130,131},{131,256},... | collective-permute-start | bytes 1544 | tf_op jit(solution)/shard_map/ppermute | solution.py:24
  868.1 4.5 collective-permute-done.73
  879.1 6.7 copy.645
  889.3 6.4 fusion.10
  899.3 4.9 reshape.360
  904.2 6.8 all-to-all-start.5
  913.0 14.5 %collective-permute-start.79 = (f32[4,1,32]{2,0,1:T(4,128)S(1)}, f32[4,1,32]{2,0,1:T(4,128)S(1)}, u32[]{:S(2)}, u32[]{:S(2)}) collective-permute-start(f32[4,1,32]{2,0,1:T(4,128)S(1)} %get-tuple-element.136), channel_id=1, source_target_pairs={{0,1},{1,2},{2,3},{3,128},{128,129},{129,130},{130,131},{131,256},... | collective-permute-start | bytes 1544 | tf_op jit(solution)/shard_map/ppermute | solution.py:24
  927.5 4.3 collective-permute-start.76
  934.3 5.2 collective-permute-done.77
  941.8 14.5 %collective-permute-start.83 = (f32[8,1,64]{2,1,0:T(1,128)S(1)}, f32[8,1,64]{2,1,0:T(1,128)S(1)}, u32[]{:S(2)}, u32[]{:S(2)}) collective-permute-start(f32[8,1,64]{2,1,0:T(1,128)S(1)} %get-tuple-element.108), channel_id=1, source_target_pairs={{0,1},{1,2},{2,3},{3,128},{128,129},{129,130},{130,131},{131,256},... | collective-permute-start | bytes 6152 | tf_op jit(solution)/shard_map/ppermute | solution.py:24
  968.0 14.5 %collective-permute-start.87 = (f32[8,1,64]{2,1,0:T(1,128)S(1)}, f32[8,1,64]{2,1,0:T(1,128)S(1)}, u32[]{:S(2)}, u32[]{:S(2)}) collective-permute-start(f32[8,1,64]{2,1,0:T(1,128)S(1)} %get-tuple-element.104), channel_id=1, source_target_pairs={{0,1},{1,2},{2,3},{3,128},{128,129},{129,130},{130,131},{131,256},... | collective-permute-start | bytes 6152 | tf_op jit(solution)/shard_map/ppermute | solution.py:24
  994.8 14.5 %collective-permute-start.91 = (f32[16,1,128]{2,1,0:T(1,128)S(1)}, f32[16,1,128]{2,1,0:T(1,128)S(1)}, u32[]{:S(2)}, u32[]{:S(2)}) collective-permute-start(f32[16,1,128]{2,1,0:T(1,128)S(1)} %get-tuple-element.68), channel_id=1, source_target_pairs={{0,1},{1,2},{2,3},{3,128},{128,129},{129,130},{130,131},{131,256},... | collective-permute-start | bytes 24584 | tf_op jit(solution)/shard_map/ppermute | solution.py:24
  1021.1 14.5 %collective-permute-start.95 = (f32[16,1,128]{2,1,0:T(1,128)S(1)}, f32[16,1,128]{2,1,0:T(1,128)S(1)}, u32[]{:S(2)}, u32[]{:S(2)}) collective-permute-start(f32[16,1,128]{2,1,0:T(1,128)S(1)} %get-tuple-element.64), channel_id=1, source_target_pairs={{0,1},{1,2},{2,3},{3,128},{128,129},{129,130},{130,131},{131,256},... | collective-permute-start | bytes 24584 | tf_op jit(solution)/shard_map/ppermute | solution.py:24
  1055.1 17.8 %fusion.8 = f32[16,32,512]{2,1,0:T(8,128)} fusion(f32[16,32,512]{1,2,0:T(8,128)S(1)} %bitcast.285), kind=kOutput, calls=%fused_computation.19 | convolution fusion | flops 1614544896 | bytes 2097152 | tf_op jit(solution)/shard_map/abj,kj->abk/dot_general | solution.py:58
  (463 shorter events, 353.0 us)
Async XLA Ops:
  14.6 58.4 %all-to-all-start.2 = ((f32[32,1,512]{2,1,0:T(1,128)}), f32[32,1,512]{2,1,0:T(1,128)S(1)}, u32[]{:S(2)}, u32[]{:S(2)}) async-start(f32[32,1,512]{2,1,0:T(1,128)} %reshape.354), calls=%async_computation.2 | async-start | bytes 131072 | tf_op jit(solution)/shard_map/all_to_all | solution.py:142
  72.9 58.3 %all-to-all-start = ((f32[32,1,8192]{2,1,0:T(1,128)}), f32[32,1,8192]{2,1,0:T(1,128)S(1)}, u32[]{:S(2)}, u32[]{:S(2)}) async-start(f32[32,1,8192]{2,1,0:T(1,128)} %reshape.350), calls=%async_computation | async-start | bytes 2097152 | tf_op jit(solution)/shard_map/all_to_all | solution.py:139
  131.2 47.3 %all-to-all-start.3 = ((f32[16,1,2048]{2,1,0:T(1,128)}), f32[16,1,2048]{2,1,0:T(1,128)S(1)}, u32[]{:S(2)}, u32[]{:S(2)}) async-start(f32[16,1,2048]{2,1,0:T(1,128)} %reshape.356), calls=%async_computation.3 | async-start | bytes 262144 | tf_op jit(solution)/shard_map/all_to_all | solution.py:148
  178.5 69.1 %all-to-all-start.1 = ((f32[16,1,16384]{2,1,0:T(1,128)}), f32[16,1,16384]{2,1,0:T(1,128)S(1)}, u32[]{:S(2)}, u32[]{:S(2)}) async-start(f32[16,1,16384]{2,1,0:T(1,128)} %reshape.352), calls=%async_computation.1 | async-start | bytes 2097152 | tf_op jit(solution)/shard_map/all_to_all | solution.py:147
  299.3 19.1 %all-to-all-start.7 = ((f32[32,1,512]{2,1,0:T(1,128)}), f32[32,1,512]{2,1,0:T(1,128)S(1)}, u32[]{:S(2)}, u32[]{:S(2)}) async-start(f32[32,1,512]{2,1,0:T(1,128)} %reshape.364), calls=%async_computation.7 | async-start | bytes 131072 | tf_op jit(solution)/shard_map/all_to_all | solution.py:168
  321.3 17.6 %collective-permute-start.1 = (f32[1,8,128]{2,1,0:T(8,128)S(1)}, f32[1,8,128]{2,1,0:T(8,128)S(1)}, u32[]{:S(2)}, u32[]{:S(2)}) collective-permute-start(f32[1,8,128]{2,1,0:T(8,128)S(1)} %copy.611), channel_id=1, source_target_pairs={{0,4},{4,8},{8,12},{12,16},{16,20},{20,24},{24,28},{28,32},{32,36}... | collective-permute-start | bytes 12296 | tf_op jit(solution)/shard_map/ppermute | solution.py:24
  324.0 15.6 %collective-permute-start = (f32[16,1,128]{2,1,0:T(1,128)S(1)}, f32[16,1,128]{2,1,0:T(1,128)S(1)}, u32[]{:S(2)}, u32[]{:S(2)}) collective-permute-start(f32[16,1,128]{2,1,0:T(1,128)S(1)} %get-tuple-element.98), channel_id=1, source_target_pairs={{0,1},{1,2},{2,3},{3,128},{128,129},{129,130},{130,131},{131,256},... | collective-permute-start | bytes 24584 | tf_op jit(solution)/shard_map/ppermute | solution.py:24
  330.6 15.8 %collective-permute-start.3 = (f32[16,1,128]{2,1,0:T(1,128)S(1)}, f32[16,1,128]{2,1,0:T(1,128)S(1)}, u32[]{:S(2)}, u32[]{:S(2)}) collective-permute-start(f32[16,1,128]{2,1,0:T(1,128)S(1)} %get-tuple-element.99), channel_id=1, source_target_pairs={{1,0},{2,1},{3,2},{128,3},{129,128},{130,129},{131,130},{256,131},... | collective-permute-start | bytes 24584 | tf_op jit(solution)/shard_map/ppermute | solution.py:25
  348.4 24.8 %collective-permute-start.6 = (f32[16,1,128]{2,1,0:T(1,128)S(1)}, f32[16,1,128]{2,1,0:T(1,128)S(1)}, u32[]{:S(2)}, u32[]{:S(2)}) collective-permute-start(f32[16,1,128]{2,1,0:T(1,128)S(1)} %get-tuple-element.97), channel_id=1, source_target_pairs={{1,0},{2,1},{3,2},{128,3},{129,128},{130,129},{131,130},{256,131},... | collective-permute-start | bytes 24584 | tf_op jit(solution)/shard_map/ppermute | solution.py:25
  350.3 22.9 %collective-permute-start.7 = (f32[16,1,128]{2,1,0:T(1,128)S(1)}, f32[16,1,128]{2,1,0:T(1,128)S(1)}, u32[]{:S(2)}, u32[]{:S(2)}) collective-permute-start(f32[16,1,128]{2,1,0:T(1,128)S(1)} %get-tuple-element.96), channel_id=1, source_target_pairs={{0,1},{1,2},{2,3},{3,128},{128,129},{129,130},{130,131},{131,256},... | collective-permute-start | bytes 24584 | tf_op jit(solution)/shard_map/ppermute | solution.py:24
  364.8 8.4 collective-permute-start.4
  379.3 21.9 %collective-permute-start.10 = (f32[16,1,128]{2,1,0:T(1,128)S(1)}, f32[16,1,128]{2,1,0:T(1,128)S(1)}, u32[]{:S(2)}, u32[]{:S(2)}) collective-permute-start(f32[16,1,128]{2,1,0:T(1,128)S(1)} %get-tuple-element.93), channel_id=1, source_target_pairs={{1,0},{2,1},{3,2},{128,3},{129,128},{130,129},{131,130},{256,131},... | collective-permute-start | bytes 24584 | tf_op jit(solution)/shard_map/ppermute | solution.py:25
  381.2 20.0 %collective-permute-start.11 = (f32[16,1,128]{2,1,0:T(1,128)S(1)}, f32[16,1,128]{2,1,0:T(1,128)S(1)}, u32[]{:S(2)}, u32[]{:S(2)}) collective-permute-start(f32[16,1,128]{2,1,0:T(1,128)S(1)} %get-tuple-element.92), channel_id=1, source_target_pairs={{0,1},{1,2},{2,3},{3,128},{128,129},{129,130},{130,131},{131,256},... | collective-permute-start | bytes 24584 | tf_op jit(solution)/shard_map/ppermute | solution.py:24
  397.8 7.7 collective-permute-start.9
  413.9 21.7 %collective-permute-start.14 = (f32[8,1,64]{2,1,0:T(1,128)S(1)}, f32[8,1,64]{2,1,0:T(1,128)S(1)}, u32[]{:S(2)}, u32[]{:S(2)}) collective-permute-start(f32[8,1,64]{2,1,0:T(1,128)S(1)} %get-tuple-element.133), channel_id=1, source_target_pairs={{1,0},{2,1},{3,2},{128,3},{129,128},{130,129},{131,130},{256,131},... | collective-permute-start | bytes 6152 | tf_op jit(solution)/shard_map/ppermute | solution.py:25
  415.8 19.8 %collective-permute-start.15 = (f32[8,1,64]{2,1,0:T(1,128)S(1)}, f32[8,1,64]{2,1,0:T(1,128)S(1)}, u32[]{:S(2)}, u32[]{:S(2)}) collective-permute-start(f32[8,1,64]{2,1,0:T(1,128)S(1)} %get-tuple-element.132), channel_id=1, source_target_pairs={{0,1},{1,2},{2,3},{3,128},{128,129},{129,130},{130,131},{131,256},... | collective-permute-start | bytes 6152 | tf_op jit(solution)/shard_map/ppermute | solution.py:24
  440.1 21.7 %collective-permute-start.18 = (f32[8,1,64]{2,1,0:T(1,128)S(1)}, f32[8,1,64]{2,1,0:T(1,128)S(1)}, u32[]{:S(2)}, u32[]{:S(2)}) collective-permute-start(f32[8,1,64]{2,1,0:T(1,128)S(1)} %get-tuple-element.129), channel_id=1, source_target_pairs={{1,0},{2,1},{3,2},{128,3},{129,128},{130,129},{131,130},{256,131},... | collective-permute-start | bytes 6152 | tf_op jit(solution)/shard_map/ppermute | solution.py:25
  442.0 19.8 %collective-permute-start.19 = (f32[8,1,64]{2,1,0:T(1,128)S(1)}, f32[8,1,64]{2,1,0:T(1,128)S(1)}, u32[]{:S(2)}, u32[]{:S(2)}) collective-permute-start(f32[8,1,64]{2,1,0:T(1,128)S(1)} %get-tuple-element.128), channel_id=1, source_target_pairs={{0,1},{1,2},{2,3},{3,128},{128,129},{129,130},{130,131},{131,256},... | collective-permute-start | bytes 6152 | tf_op jit(solution)/shard_map/ppermute | solution.py:24
  467.0 21.7 %collective-permute-start.22 = (f32[4,1,32]{2,0,1:T(4,128)S(1)}, f32[4,1,32]{2,0,1:T(4,128)S(1)}, u32[]{:S(2)}, u32[]{:S(2)}) collective-permute-start(f32[4,1,32]{2,0,1:T(4,128)S(1)} %get-tuple-element.157), channel_id=1, source_target_pairs={{1,0},{2,1},{3,2},{128,3},{129,128},{130,129},{131,130},{256,131},... | collective-permute-start | bytes 1544 | tf_op jit(solution)/shard_map/ppermute | solution.py:25
  468.9 19.8 %collective-permute-start.23 = (f32[4,1,32]{2,0,1:T(4,128)S(1)}, f32[4,1,32]{2,0,1:T(4,128)S(1)}, u32[]{:S(2)}, u32[]{:S(2)}) collective-permute-start(f32[4,1,32]{2,0,1:T(4,128)S(1)} %get-tuple-element.156), channel_id=1, source_target_pairs={{0,1},{1,2},{2,3},{3,128},{128,129},{129,130},{130,131},{131,256},... | collective-permute-start | bytes 1544 | tf_op jit(solution)/shard_map/ppermute | solution.py:24
  493.1 21.7 %collective-permute-start.26 = (f32[4,1,32]{2,0,1:T(4,128)S(1)}, f32[4,1,32]{2,0,1:T(4,128)S(1)}, u32[]{:S(2)}, u32[]{:S(2)}) collective-permute-start(f32[4,1,32]{2,0,1:T(4,128)S(1)} %get-tuple-element.153), channel_id=1, source_target_pairs={{1,0},{2,1},{3,2},{128,3},{129,128},{130,129},{131,130},{256,131},... | collective-permute-start | bytes 1544 | tf_op jit(solution)/shard_map/ppermute | solution.py:25
  495.1 19.8 %collective-permute-start.27 = (f32[4,1,32]{2,0,1:T(4,128)S(1)}, f32[4,1,32]{2,0,1:T(4,128)S(1)}, u32[]{:S(2)}, u32[]{:S(2)}) collective-permute-start(f32[4,1,32]{2,0,1:T(4,128)S(1)} %get-tuple-element.152), channel_id=1, source_target_pairs={{0,1},{1,2},{2,3},{3,128},{128,129},{129,130},{130,131},{131,256},... | collective-permute-start | bytes 1544 | tf_op jit(solution)/shard_map/ppermute | solution.py:24
  519.3 21.7 %collective-permute-start.30 = (f32[4,1,32]{2,0,1:T(4,128)S(1)}, f32[4,1,32]{2,0,1:T(4,128)S(1)}, u32[]{:S(2)}, u32[]{:S(2)}) collective-permute-start(f32[4,1,32]{2,0,1:T(4,128)S(1)} %get-tuple-element.149), channel_id=1, source_target_pairs={{1,0},{2,1},{3,2},{128,3},{129,128},{130,129},{131,130},{256,131},... | collective-permute-start | bytes 1544 | tf_op jit(solution)/shard_map/ppermute | solution.py:25
  521.2 19.8 %collective-permute-start.31 = (f32[4,1,32]{2,0,1:T(4,128)S(1)}, f32[4,1,32]{2,0,1:T(4,128)S(1)}, u32[]{:S(2)}, u32[]{:S(2)}) collective-permute-start(f32[4,1,32]{2,0,1:T(4,128)S(1)} %get-tuple-element.148), channel_id=1, source_target_pairs={{0,1},{1,2},{2,3},{3,128},{128,129},{129,130},{130,131},{131,256},... | collective-permute-start | bytes 1544 | tf_op jit(solution)/shard_map/ppermute | solution.py:24
  545.7 21.7 %collective-permute-start.34 = (f32[8,1,64]{2,1,0:T(1,128)S(1)}, f32[8,1,64]{2,1,0:T(1,128)S(1)}, u32[]{:S(2)}, u32[]{:S(2)}) collective-permute-start(f32[8,1,64]{2,1,0:T(1,128)S(1)} %get-tuple-element.125), channel_id=1, source_target_pairs={{1,0},{2,1},{3,2},{128,3},{129,128},{130,129},{131,130},{256,131},... | collective-permute-start | bytes 6152 | tf_op jit(solution)/shard_map/ppermute | solution.py:25
  547.6 19.8 %collective-permute-start.35 = (f32[8,1,64]{2,1,0:T(1,128)S(1)}, f32[8,1,64]{2,1,0:T(1,128)S(1)}, u32[]{:S(2)}, u32[]{:S(2)}) collective-permute-start(f32[8,1,64]{2,1,0:T(1,128)S(1)} %get-tuple-element.124), channel_id=1, source_target_pairs={{0,1},{1,2},{2,3},{3,128},{128,129},{129,130},{130,131},{131,256},... | collective-permute-start | bytes 6152 | tf_op jit(solution)/shard_map/ppermute | solution.py:24
  571.9 21.7 %collective-permute-start.38 = (f32[8,1,64]{2,1,0:T(1,128)S(1)}, f32[8,1,64]{2,1,0:T(1,128)S(1)}, u32[]{:S(2)}, u32[]{:S(2)}) collective-permute-start(f32[8,1,64]{2,1,0:T(1,128)S(1)} %get-tuple-element.121), channel_id=1, source_target_pairs={{1,0},{2,1},{3,2},{128,3},{129,128},{130,129},{131,130},{256,131},... | collective-permute-start | bytes 6152 | tf_op jit(solution)/shard_map/ppermute | solution.py:25
  573.8 19.8 %collective-permute-start.39 = (f32[8,1,64]{2,1,0:T(1,128)S(1)}, f32[8,1,64]{2,1,0:T(1,128)S(1)}, u32[]{:S(2)}, u32[]{:S(2)}) collective-permute-start(f32[8,1,64]{2,1,0:T(1,128)S(1)} %get-tuple-element.120), channel_id=1, source_target_pairs={{0,1},{1,2},{2,3},{3,128},{128,129},{129,130},{130,131},{131,256},... | collective-permute-start | bytes 6152 | tf_op jit(solution)/shard_map/ppermute | solution.py:24
  598.6 21.7 %collective-permute-start.42 = (f32[16,1,128]{2,1,0:T(1,128)S(1)}, f32[16,1,128]{2,1,0:T(1,128)S(1)}, u32[]{:S(2)}, u32[]{:S(2)}) collective-permute-start(f32[16,1,128]{2,1,0:T(1,128)S(1)} %get-tuple-element.89), channel_id=1, source_target_pairs={{1,0},{2,1},{3,2},{128,3},{129,128},{130,129},{131,130},{256,131},... | collective-permute-start | bytes 24584 | tf_op jit(solution)/shard_map/ppermute | solution.py:25
  600.5 19.8 %collective-permute-start.43 = (f32[16,1,128]{2,1,0:T(1,128)S(1)}, f32[16,1,128]{2,1,0:T(1,128)S(1)}, u32[]{:S(2)}, u32[]{:S(2)}) collective-permute-start(f32[16,1,128]{2,1,0:T(1,128)S(1)} %get-tuple-element.88), channel_id=1, source_target_pairs={{0,1},{1,2},{2,3},{3,128},{128,129},{129,130},{130,131},{131,256},... | collective-permute-start | bytes 24584 | tf_op jit(solution)/shard_map/ppermute | solution.py:24
  625.0 21.7 %collective-permute-start.46 = (f32[16,1,128]{2,1,0:T(1,128)S(1)}, f32[16,1,128]{2,1,0:T(1,128)S(1)}, u32[]{:S(2)}, u32[]{:S(2)}) collective-permute-start(f32[16,1,128]{2,1,0:T(1,128)S(1)} %get-tuple-element.85), channel_id=1, source_target_pairs={{1,0},{2,1},{3,2},{128,3},{129,128},{130,129},{131,130},{256,131},... | collective-permute-start | bytes 24584 | tf_op jit(solution)/shard_map/ppermute | solution.py:25
  626.9 19.8 %collective-permute-start.47 = (f32[16,1,128]{2,1,0:T(1,128)S(1)}, f32[16,1,128]{2,1,0:T(1,128)S(1)}, u32[]{:S(2)}, u32[]{:S(2)}) collective-permute-start(f32[16,1,128]{2,1,0:T(1,128)S(1)} %get-tuple-element.84), channel_id=1, source_target_pairs={{0,1},{1,2},{2,3},{3,128},{128,129},{129,130},{130,131},{131,256},... | collective-permute-start | bytes 24584 | tf_op jit(solution)/shard_map/ppermute | solution.py:24
  651.3 21.7 %collective-permute-start.50 = (f32[16,1,128]{2,1,0:T(1,128)S(1)}, f32[16,1,128]{2,1,0:T(1,128)S(1)}, u32[]{:S(2)}, u32[]{:S(2)}) collective-permute-start(f32[16,1,128]{2,1,0:T(1,128)S(1)} %get-tuple-element.81), channel_id=1, source_target_pairs={{1,0},{2,1},{3,2},{128,3},{129,128},{130,129},{131,130},{256,131},... | collective-permute-start | bytes 24584 | tf_op jit(solution)/shard_map/ppermute | solution.py:25
  653.3 19.8 %collective-permute-start.51 = (f32[16,1,128]{2,1,0:T(1,128)S(1)}, f32[16,1,128]{2,1,0:T(1,128)S(1)}, u32[]{:S(2)}, u32[]{:S(2)}) collective-permute-start(f32[16,1,128]{2,1,0:T(1,128)S(1)} %get-tuple-element.80), channel_id=1, source_target_pairs={{0,1},{1,2},{2,3},{3,128},{128,129},{129,130},{130,131},{131,256},... | collective-permute-start | bytes 24584 | tf_op jit(solution)/shard_map/ppermute | solution.py:24
  677.7 41.3 %collective-permute-start.54 = (f32[16,1,128]{2,1,0:T(1,128)S(1)}, f32[16,1,128]{2,1,0:T(1,128)S(1)}, u32[]{:S(2)}, u32[]{:S(2)}) collective-permute-start(f32[16,1,128]{2,1,0:T(1,128)S(1)} %get-tuple-element.77), channel_id=1, source_target_pairs={{1,0},{2,1},{3,2},{128,3},{129,128},{130,129},{131,130},{256,131},... | collective-permute-start | bytes 24584 | tf_op jit(solution)/shard_map/ppermute | solution.py:25
  679.6 39.4 %collective-permute-start.55 = (f32[16,1,128]{2,1,0:T(1,128)S(1)}, f32[16,1,128]{2,1,0:T(1,128)S(1)}, u32[]{:S(2)}, u32[]{:S(2)}) collective-permute-start(f32[16,1,128]{2,1,0:T(1,128)S(1)} %get-tuple-element.76), channel_id=1, source_target_pairs={{0,1},{1,2},{2,3},{3,128},{128,129},{129,130},{130,131},{131,256},... | collective-permute-start | bytes 24584 | tf_op jit(solution)/shard_map/ppermute | solution.py:24
  694.1 24.9 %collective-permute-start.52 = (f32[1,8,128]{2,1,0:T(8,128)S(1)}, f32[1,8,128]{2,1,0:T(8,128)S(1)}, u32[]{:S(2)}, u32[]{:S(2)}) collective-permute-start(f32[1,8,128]{2,1,0:T(8,128)S(1)} %get-tuple-element.75), channel_id=1, source_target_pairs={{4,0},{8,4},{12,8},{16,12},{20,16},{24,20},{28,24},{32,28},{36,32}... | collective-permute-start | bytes 12296 | tf_op jit(solution)/shard_map/ppermute | solution.py:25
  696.0 23.0 %collective-permute-start.53 = (f32[1,8,128]{2,1,0:T(8,128)S(1)}, f32[1,8,128]{2,1,0:T(8,128)S(1)}, u32[]{:S(2)}, u32[]{:S(2)}) collective-permute-start(f32[1,8,128]{2,1,0:T(8,128)S(1)} %get-tuple-element.74), channel_id=1, source_target_pairs={{0,4},{4,8},{8,12},{12,16},{16,20},{20,24},{24,28},{28,32},{32,36}... | collective-permute-start | bytes 12296 | tf_op jit(solution)/shard_map/ppermute | solution.py:24
  714.7 158.0 %all-to-all-start.4 = ((f32[16,1,16384]{2,1,0:T(1,128)}), f32[16,1,16384]{2,1,0:T(1,128)S(1)}, u32[]{:S(2)}, u32[]{:S(2)}) async-start(f32[16,1,16384]{2,1,0:T(1,128)} %reshape.358), calls=%async_computation.4 | async-start | bytes 2097152 | tf_op jit(solution)/shard_map/all_to_all | solution.py:161
  719.4 24.1 %collective-permute-start.58 = (f32[16,1,128]{2,1,0:T(1,128)S(1)}, f32[16,1,128]{2,1,0:T(1,128)S(1)}, u32[]{:S(2)}, u32[]{:S(2)}) collective-permute-start(f32[16,1,128]{2,1,0:T(1,128)S(1)} %get-tuple-element.73), channel_id=1, source_target_pairs={{1,0},{2,1},{3,2},{128,3},{129,128},{130,129},{131,130},{256,131},... | collective-permute-start | bytes 24584 | tf_op jit(solution)/shard_map/ppermute | solution.py:25
  721.9 21.6 %collective-permute-start.59 = (f32[16,1,128]{2,1,0:T(1,128)S(1)}, f32[16,1,128]{2,1,0:T(1,128)S(1)}, u32[]{:S(2)}, u32[]{:S(2)}) collective-permute-start(f32[16,1,128]{2,1,0:T(1,128)S(1)} %get-tuple-element.72), channel_id=1, source_target_pairs={{0,1},{1,2},{2,3},{3,128},{128,129},{129,130},{130,131},{131,256},... | collective-permute-start | bytes 24584 | tf_op jit(solution)/shard_map/ppermute | solution.py:24
  735.8 7.7 collective-permute-start.56
  741.0 8.1 collective-permute-start.57
  757.6 21.7 %collective-permute-start.62 = (f32[8,1,64]{2,1,0:T(1,128)S(1)}, f32[8,1,64]{2,1,0:T(1,128)S(1)}, u32[]{:S(2)}, u32[]{:S(2)}) collective-permute-start(f32[8,1,64]{2,1,0:T(1,128)S(1)} %get-tuple-element.117), channel_id=1, source_target_pairs={{1,0},{2,1},{3,2},{128,3},{129,128},{130,129},{131,130},{256,131},... | collective-permute-start | bytes 6152 | tf_op jit(solution)/shard_map/ppermute | solution.py:25
  759.5 19.8 %collective-permute-start.63 = (f32[8,1,64]{2,1,0:T(1,128)S(1)}, f32[8,1,64]{2,1,0:T(1,128)S(1)}, u32[]{:S(2)}, u32[]{:S(2)}) collective-permute-start(f32[8,1,64]{2,1,0:T(1,128)S(1)} %get-tuple-element.116), channel_id=1, source_target_pairs={{0,1},{1,2},{2,3},{3,128},{128,129},{129,130},{130,131},{131,256},... | collective-permute-start | bytes 6152 | tf_op jit(solution)/shard_map/ppermute | solution.py:24
  775.9 15.1 %collective-permute-start.61 = (f32[1,4,64]{2,1,0:T(4,128)S(1)}, f32[1,4,64]{2,1,0:T(4,128)S(1)}, u32[]{:S(2)}, u32[]{:S(2)}) collective-permute-start(f32[1,4,64]{2,1,0:T(4,128)S(1)} %get-tuple-element.114), channel_id=1, source_target_pairs={{0,4},{4,8},{8,12},{12,16},{16,20},{20,24},{24,28},{28,32},{32,36}... | collective-permute-start | bytes 3080 | tf_op jit(solution)/shard_map/ppermute | solution.py:24
  791.2 22.4 %collective-permute-start.66 = (f32[8,1,64]{2,1,0:T(1,128)S(1)}, f32[8,1,64]{2,1,0:T(1,128)S(1)}, u32[]{:S(2)}, u32[]{:S(2)}) collective-permute-start(f32[8,1,64]{2,1,0:T(1,128)S(1)} %get-tuple-element.113), channel_id=1, source_target_pairs={{1,0},{2,1},{3,2},{128,3},{129,128},{130,129},{131,130},{256,131},... | collective-permute-start | bytes 6152 | tf_op jit(solution)/shard_map/ppermute | solution.py:25
  793.2 20.5 %collective-permute-start.67 = (f32[8,1,64]{2,1,0:T(1,128)S(1)}, f32[8,1,64]{2,1,0:T(1,128)S(1)}, u32[]{:S(2)}, u32[]{:S(2)}) collective-permute-start(f32[8,1,64]{2,1,0:T(1,128)S(1)} %get-tuple-element.112), channel_id=1, source_target_pairs={{0,1},{1,2},{2,3},{3,128},{128,129},{129,130},{130,131},{131,256},... | collective-permute-start | bytes 6152 | tf_op jit(solution)/shard_map/ppermute | solution.py:24
  820.2 21.7 %collective-permute-start.70 = (f32[4,1,32]{2,0,1:T(4,128)S(1)}, f32[4,1,32]{2,0,1:T(4,128)S(1)}, u32[]{:S(2)}, u32[]{:S(2)}) collective-permute-start(f32[4,1,32]{2,0,1:T(4,128)S(1)} %get-tuple-element.145), channel_id=1, source_target_pairs={{1,0},{2,1},{3,2},{128,3},{129,128},{130,129},{131,130},{256,131},... | collective-permute-start | bytes 1544 | tf_op jit(solution)/shard_map/ppermute | solution.py:25
  822.1 19.8 %collective-permute-start.71 = (f32[4,1,32]{2,0,1:T(4,128)S(1)}, f32[4,1,32]{2,0,1:T(4,128)S(1)}, u32[]{:S(2)}, u32[]{:S(2)}) collective-permute-start(f32[4,1,32]{2,0,1:T(4,128)S(1)} %get-tuple-element.144), channel_id=1, source_target_pairs={{0,1},{1,2},{2,3},{3,128},{128,129},{129,130},{130,131},{131,256},... | collective-permute-start | bytes 1544 | tf_op jit(solution)/shard_map/ppermute | solution.py:24
  846.4 21.7 %collective-permute-start.74 = (f32[4,1,32]{2,0,1:T(4,128)S(1)}, f32[4,1,32]{2,0,1:T(4,128)S(1)}, u32[]{:S(2)}, u32[]{:S(2)}) collective-permute-start(f32[4,1,32]{2,0,1:T(4,128)S(1)} %get-tuple-element.141), channel_id=1, source_target_pairs={{1,0},{2,1},{3,2},{128,3},{129,128},{130,129},{131,130},{256,131},... | collective-permute-start | bytes 1544 | tf_op jit(solution)/shard_map/ppermute | solution.py:25
  848.3 19.8 %collective-permute-start.75 = (f32[4,1,32]{2,0,1:T(4,128)S(1)}, f32[4,1,32]{2,0,1:T(4,128)S(1)}, u32[]{:S(2)}, u32[]{:S(2)}) collective-permute-start(f32[4,1,32]{2,0,1:T(4,128)S(1)} %get-tuple-element.140), channel_id=1, source_target_pairs={{0,1},{1,2},{2,3},{3,128},{128,129},{129,130},{130,131},{131,256},... | collective-permute-start | bytes 1544 | tf_op jit(solution)/shard_map/ppermute | solution.py:24
  864.7 7.9 collective-permute-start.73
  904.2 141.9 %all-to-all-start.5 = ((f32[32,1,8192]{2,1,0:T(1,128)}), f32[32,1,8192]{2,1,0:T(1,128)S(1)}, u32[]{:S(2)}, u32[]{:S(2)}) async-start(f32[32,1,8192]{2,1,0:T(1,128)} %reshape.360), calls=%async_computation.5 | async-start | bytes 2097152 | tf_op jit(solution)/shard_map/all_to_all | solution.py:167
  911.1 22.6 %collective-permute-start.78 = (f32[4,1,32]{2,0,1:T(4,128)S(1)}, f32[4,1,32]{2,0,1:T(4,128)S(1)}, u32[]{:S(2)}, u32[]{:S(2)}) collective-permute-start(f32[4,1,32]{2,0,1:T(4,128)S(1)} %get-tuple-element.137), channel_id=1, source_target_pairs={{1,0},{2,1},{3,2},{128,3},{129,128},{130,129},{131,130},{256,131},... | collective-permute-start | bytes 1544 | tf_op jit(solution)/shard_map/ppermute | solution.py:25
  913.0 20.8 %collective-permute-start.79 = (f32[4,1,32]{2,0,1:T(4,128)S(1)}, f32[4,1,32]{2,0,1:T(4,128)S(1)}, u32[]{:S(2)}, u32[]{:S(2)}) collective-permute-start(f32[4,1,32]{2,0,1:T(4,128)S(1)} %get-tuple-element.136), channel_id=1, source_target_pairs={{0,1},{1,2},{2,3},{3,128},{128,129},{129,130},{130,131},{131,256},... | collective-permute-start | bytes 1544 | tf_op jit(solution)/shard_map/ppermute | solution.py:24
  939.9 21.7 %collective-permute-start.82 = (f32[8,1,64]{2,1,0:T(1,128)S(1)}, f32[8,1,64]{2,1,0:T(1,128)S(1)}, u32[]{:S(2)}, u32[]{:S(2)}) collective-permute-start(f32[8,1,64]{2,1,0:T(1,128)S(1)} %get-tuple-element.109), channel_id=1, source_target_pairs={{1,0},{2,1},{3,2},{128,3},{129,128},{130,129},{131,130},{256,131},... | collective-permute-start | bytes 6152 | tf_op jit(solution)/shard_map/ppermute | solution.py:25
  941.8 19.8 %collective-permute-start.83 = (f32[8,1,64]{2,1,0:T(1,128)S(1)}, f32[8,1,64]{2,1,0:T(1,128)S(1)}, u32[]{:S(2)}, u32[]{:S(2)}) collective-permute-start(f32[8,1,64]{2,1,0:T(1,128)S(1)} %get-tuple-element.108), channel_id=1, source_target_pairs={{0,1},{1,2},{2,3},{3,128},{128,129},{129,130},{130,131},{131,256},... | collective-permute-start | bytes 6152 | tf_op jit(solution)/shard_map/ppermute | solution.py:24
  966.1 21.7 %collective-permute-start.86 = (f32[8,1,64]{2,1,0:T(1,128)S(1)}, f32[8,1,64]{2,1,0:T(1,128)S(1)}, u32[]{:S(2)}, u32[]{:S(2)}) collective-permute-start(f32[8,1,64]{2,1,0:T(1,128)S(1)} %get-tuple-element.105), channel_id=1, source_target_pairs={{1,0},{2,1},{3,2},{128,3},{129,128},{130,129},{131,130},{256,131},... | collective-permute-start | bytes 6152 | tf_op jit(solution)/shard_map/ppermute | solution.py:25
  968.0 19.8 %collective-permute-start.87 = (f32[8,1,64]{2,1,0:T(1,128)S(1)}, f32[8,1,64]{2,1,0:T(1,128)S(1)}, u32[]{:S(2)}, u32[]{:S(2)}) collective-permute-start(f32[8,1,64]{2,1,0:T(1,128)S(1)} %get-tuple-element.104), channel_id=1, source_target_pairs={{0,1},{1,2},{2,3},{3,128},{128,129},{129,130},{130,131},{131,256},... | collective-permute-start | bytes 6152 | tf_op jit(solution)/shard_map/ppermute | solution.py:24
  992.8 21.7 %collective-permute-start.90 = (f32[16,1,128]{2,1,0:T(1,128)S(1)}, f32[16,1,128]{2,1,0:T(1,128)S(1)}, u32[]{:S(2)}, u32[]{:S(2)}) collective-permute-start(f32[16,1,128]{2,1,0:T(1,128)S(1)} %get-tuple-element.69), channel_id=1, source_target_pairs={{1,0},{2,1},{3,2},{128,3},{129,128},{130,129},{131,130},{256,131},... | collective-permute-start | bytes 24584 | tf_op jit(solution)/shard_map/ppermute | solution.py:25
  994.8 19.8 %collective-permute-start.91 = (f32[16,1,128]{2,1,0:T(1,128)S(1)}, f32[16,1,128]{2,1,0:T(1,128)S(1)}, u32[]{:S(2)}, u32[]{:S(2)}) collective-permute-start(f32[16,1,128]{2,1,0:T(1,128)S(1)} %get-tuple-element.68), channel_id=1, source_target_pairs={{0,1},{1,2},{2,3},{3,128},{128,129},{129,130},{130,131},{131,256},... | collective-permute-start | bytes 24584 | tf_op jit(solution)/shard_map/ppermute | solution.py:24
  1019.2 21.7 %collective-permute-start.94 = (f32[16,1,128]{2,1,0:T(1,128)S(1)}, f32[16,1,128]{2,1,0:T(1,128)S(1)}, u32[]{:S(2)}, u32[]{:S(2)}) collective-permute-start(f32[16,1,128]{2,1,0:T(1,128)S(1)} %get-tuple-element.65), channel_id=1, source_target_pairs={{1,0},{2,1},{3,2},{128,3},{129,128},{130,129},{131,130},{256,131},... | collective-permute-start | bytes 24584 | tf_op jit(solution)/shard_map/ppermute | solution.py:25
  1021.1 19.8 %collective-permute-start.95 = (f32[16,1,128]{2,1,0:T(1,128)S(1)}, f32[16,1,128]{2,1,0:T(1,128)S(1)}, u32[]{:S(2)}, u32[]{:S(2)}) collective-permute-start(f32[16,1,128]{2,1,0:T(1,128)S(1)} %get-tuple-element.64), channel_id=1, source_target_pairs={{0,1},{1,2},{2,3},{3,128},{128,129},{129,130},{130,131},{131,256},... | collective-permute-start | bytes 24584 | tf_op jit(solution)/shard_map/ppermute | solution.py:24
  (43 other events, 401.2 us)
